TPU v7x, 256 devices: a whole 4x4x8 slice. The times are simulated.
256 devices in a mesh: cls: 64 (over x, z, y_lo), dp: 4 (over y_hi, core).
Axes of the slice: x: 4, y: 4 (y_hi: 2, y_lo: 2; y = y_hi * 2 + y_lo), z: 8, core: 2. Of those that a mesh axis runs over, the one named last changes fastest.
Arguments:
- embeddings: bfloat16 [2048, 512], P(('dp', 'cls')), parts along dimension 0, may hold values from -4.4194174 to 4.4194174
- labels: int32 [2048], P(('dp', 'cls')), parts along dimension 0, may hold values from 0 to 262143
- centers: bfloat16 [1048576, 512], P(('dp', 'cls')), parts along dimension 0, may hold values from -3.0935922 to 3.0935922
Outputs:
- losses: float32 [2048], P(('dp', 'cls')), parts along dimension 0
- emb_grad: float32 [2048, 512], P(('dp', 'cls')), parts along dimension 0
- center_grad: float32 [1048576, 512], P(('dp', 'cls')), parts along dimension 0
There are 4 independent parts, one for each index of `dp`. A program takes and returns all parts, laid end to end along the dimension named above; each array names one. Nothing has to cross between parts.
All inputs are finite; a program needn't handle non-finite values.
Results may differ from a plain program's by a relative error of at most 0.0042.
Values may be sent and summed in bfloat16 or wider, within the bound.
No kernel may reach another device: no remote copies, remote signals or barrier semaphores. Data moves between devices by JAX's collectives and lax.ppermute only.
A program may use at most 64 MiB of HBM per device.

v0:
```python
import math

import jax
import jax.numpy as jnp
from jax import lax
from jax.sharding import PartitionSpec as P

logit_scale = 64.0
margin_cosine = math.cos(0.5)
margin_sine = math.sin(0.5)
sine_soften = 0.04
norm_eps = 1e-06


def from_everyone(shard, axis):
    peers = lax.axis_size(axis)
    return lax.all_to_all(
        jnp.broadcast_to(shard[None], (peers, *shard.shape)), axis, 0, 0, tiled=True
    )


def in_order(blocks, dim):
    blocks = jnp.moveaxis(blocks, 0, dim)
    dims = blocks.shape
    return blocks.reshape(*dims[:dim], dims[dim] * dims[dim + 1], *dims[dim + 2 :])


def gathered_copies(shard, axis, dim):
    blocks = from_everyone(shard, axis)
    return in_order(blocks, dim)


def over_copies(shard, axis):
    return from_everyone(shard, axis).sum(axis=0)


def packed_total(arrays, axis):
    ends = [0]
    for a in arrays:
        ends.append(ends[-1] + a.size)
    subtotal = over_copies(jnp.concatenate([a.ravel() for a in arrays]), axis)
    return tuple((subtotal[b:e].reshape(a.shape) for a, b, e in zip(arrays, ends, ends[1:])))


def split_up(shard, dim, peers):
    dims = shard.shape
    blocks = shard.reshape(*dims[:dim], peers, dims[dim] // peers, *dims[dim + 1 :])
    return jnp.moveaxis(blocks, dim, 0)


def sum_at_owner(shard, axis, dim):
    blocks = split_up(shard, dim, lax.axis_size(axis))
    arrived = lax.all_to_all(blocks, axis, split_axis=0, concat_axis=0, tiled=True)
    return arrived.astype(jnp.float32).sum(axis=0)


def unit_rows(values):
    widened = values.astype(jnp.float32)
    inverse = lax.rsqrt(jnp.sum(widened * widened, axis=1, keepdims=True) + norm_eps)
    normed = widened * inverse
    return (inverse, normed, normed.astype(jnp.bfloat16))


def score_block(rows_hat, rows_label, center_block, class_base):
    cosine = jnp.dot(rows_hat, center_block.T, preferred_element_type=jnp.float32)
    local_col = rows_label - class_base
    is_owned = (local_col >= 0) & (local_col < center_block.shape[0])
    column = lax.broadcasted_iota(jnp.int32, cosine.shape, 1)
    target_mask = column == local_col[:, None]
    target_cos = jnp.sum(jnp.where(target_mask, cosine, 0.0), axis=1)
    target_sine = jnp.sqrt(1.0 + sine_soften - target_cos * target_cos)
    shifted = target_cos * margin_cosine - target_sine * margin_sine
    slopes = margin_cosine + margin_sine * target_cos / target_sine
    logits = jnp.where(target_mask, logit_scale * shifted[:, None], logit_scale * cosine)
    exp_terms = jnp.exp(logits - logit_scale)
    row_total = jnp.sum(exp_terms, axis=1)
    weighted = (logit_scale * exp_terms * jnp.where(target_mask, slopes[:, None], 1.0)).astype(
        jnp.bfloat16
    )
    target = jnp.where(is_owned, logit_scale * shifted, 0.0)
    columns = jnp.where(is_owned, local_col, -1).astype(jnp.int32)
    return (weighted, row_total, target, columns, jnp.where(is_owned, slopes, 0.0))


def row_term(weighted, center_block, totals, columns, slopes):
    product = jnp.dot(weighted, center_block, preferred_element_type=jnp.float32)
    picked = jnp.take(center_block, jnp.clip(columns, 0, center_block.shape[0] - 1), axis=0).astype(
        jnp.float32
    )
    return product / totals[:, None] - (logit_scale * slopes)[:, None] * picked


def class_term(weighted, scaled, rows_hat, columns, slopes, class_count):
    product = lax.dot_general(
        weighted, scaled, (((0,), (0,)), ((), ())), preferred_element_type=jnp.float32
    )
    drop_index = jnp.where(columns >= 0, columns, class_count)
    updates = -(logit_scale * slopes)[:, None] * rows_hat.astype(jnp.float32)
    return product.at[drop_index].add(updates, mode="drop")


def take_rows(whole, first_row, row_count):
    return lax.dynamic_slice_in_dim(whole, first_row, row_count, 0)


def per_device(embeddings, labels, centers):
    own_rows = embeddings.shape[0]
    class_count = centers.shape[0]
    class_base = lax.axis_index("cls") * class_count
    own_start = lax.axis_index("cls") * own_rows
    inv_x, units_x, emb_hat = unit_rows(embeddings)
    inv_w, units_w, center_hat = unit_rows(centers)
    rows_hat = gathered_copies(emb_hat, "cls", 0)
    rows_label = gathered_copies(labels, "cls", 0)
    weighted, row_total, target, columns, slopes = score_block(
        rows_hat, rows_label, center_hat, class_base
    )
    totals = row_total
    targets = target
    totals_all, targets_all = packed_total((totals, targets), "cls")
    own_total = take_rows(totals_all, own_start, own_rows)
    own_target = take_rows(targets_all, own_start, own_rows)
    losses = jnp.log(own_total) + logit_scale - own_target
    rows_hat = gathered_copies(emb_hat, "cls", 0)
    rows_label = gathered_copies(labels, "cls", 0)
    row_count = rows_hat.shape[0]
    weighted, row_total, target, columns, slopes = score_block(
        rows_hat, rows_label, center_hat, class_base
    )
    piece_totals = take_rows(totals_all, jnp.int32(0), row_count)
    scaled = (rows_hat.astype(jnp.float32) / piece_totals[:, None]).astype(jnp.bfloat16)
    grads_hat = class_term(weighted, scaled, rows_hat, columns, slopes, class_count)
    rows_out = row_term(weighted, center_hat, piece_totals, columns, slopes)
    grad_hat_w, rows_out = (grads_hat, rows_out)
    grad_hat_x = sum_at_owner(rows_out.astype(jnp.bfloat16), "cls", 0)
    emb_grad = inv_x * (grad_hat_x - units_x * jnp.sum(units_x * grad_hat_x, axis=1, keepdims=True))
    center_grad = inv_w * (
        grad_hat_w - units_w * jnp.sum(units_w * grad_hat_w, axis=1, keepdims=True)
    )
    return (losses, emb_grad, center_grad)


def solution(mesh):
    in_specs = (P(("dp", "cls"), None), P(("dp", "cls")), P(("dp", "cls"), None))
    out_specs = (P(("dp", "cls")), P(("dp", "cls"), None), P(("dp", "cls"), None))
    return jax.shard_map(
        per_device, mesh=mesh, in_specs=in_specs, out_specs=out_specs, check_vma=False
    )
```

profile of v0, /device:TPU:16, one launch (start us, length us, event | category | flops | bytes accessed | tf_op | source)
XLA Modules:
  0.0 122.2 jit_solution(4518268095324731753)
XLA Ops:
  0.6 1.3 %broadcast_in_dim.56 = s32[64,1,8]{2,1,0:T(1,128)} broadcast(s32[8]{0:T(128)} %param.4), dimensions={2} | broadcast | bytes 2080 | tf_op jit(solution)/shard_map/broadcast_in_dim | solution.py:18
  1.9 12.7 %all-to-all-start = ((s32[64,1,8]{2,1,0:T(1,128)}), s32[64,1,8]{2,1,0:T(1,128)S(1)}, u32[]{:S(2)}, u32[]{:S(2)}) async-start(s32[64,1,8]{2,1,0:T(1,128)} %broadcast_in_dim.56), calls=%async_computation | async-start | bytes 65536 | tf_op jit(solution)/shard_map/all_to_all | solution.py:17
  14.6 3.1 %fusion.6 = f32[4096]{0:T(1024)S(1)} fusion(bf16[4096,512]{1,0:T(8,128)(2,1)} %param.5), kind=kLoop, calls=%fused_computation.10 | loop fusion | flops 6287360 | bytes 4210688 | tf_op jit(solution)/shard_map/reduce_sum | solution.py:59
  17.7 0.8 fusion.27
  18.5 0.8 fusion.23
  19.3 5.6 %all-to-all-done = s32[64,1,8]{2,1,0:T(1,128)S(1)} async-done(((s32[64,1,8]{2,1,0:T(1,128)}), s32[64,1,8]{2,1,0:T(1,128)S(1)}, u32[]{:S(2)}, u32[]{:S(2)}) %all-to-all-start) | async-done | bytes 2080 | tf_op jit(solution)/shard_map/all_to_all | solution.py:17
  24.9 0.8 broadcast_in_dim.57
  25.7 5.6 %all-to-all-start.1 = ((bf16[64,8,512]{2,1,0:T(8,128)(2,1)}), bf16[64,8,512]{2,1,0:T(8,128)(2,1)S(1)}, u32[]{:S(2)}, u32[]{:S(2)}) async-start(bf16[64,8,512]{2,1,0:T(8,128)(2,1)} %broadcast_in_dim.57), calls=%async_computation.1 | async-start | bytes 1048576 | tf_op jit(solution)/shard_map/all_to_all | solution.py:17
  31.3 4.1 %fusion.2 = bf16[4096,512]{1,0:T(8,128)(2,1)} fusion(bf16[4096,512]{1,0:T(8,128)(2,1)} %param.5, f32[4096]{0:T(1024)S(1)} %add_rsqrt_fusion), kind=kLoop, calls=%fused_computation.6 | loop fusion | flops 6291456 | bytes 8404992 | tf_op jit(solution)/shard_map/convert_element_type | solution.py:61
  35.4 0.5 broadcast.341
  35.9 0.7 fusion.29
  36.7 0.1 sub.79
  36.8 0.1 sub.84
  36.8 11.6 %all-to-all-done.1 = bf16[64,8,512]{2,1,0:T(8,128)(2,1)S(1)} async-done(((bf16[64,8,512]{2,1,0:T(8,128)(2,1)}), bf16[64,8,512]{2,1,0:T(8,128)(2,1)S(1)}, u32[]{:S(2)}, u32[]{:S(2)}) %all-to-all-start.1) | async-done | bytes 524320 | tf_op jit(solution)/shard_map/all_to_all | solution.py:17
  48.5 4.7 %select_reduce_fusion = (f32[512]{0:T(512)S(1)}, f32[512,4096]{1,0:T(8,128)S(1)}) fusion(s32[512]{0:T(512)S(1)} %sub.79, bf16[4096,512]{1,0:T(8,128)(2,1)} %fusion.2, bf16[64,8,512]{2,1,0:T(8,128)(2,1)S(1)} %all-to-all-done.1), kind=kOutput, calls=%fused_computation.13 | convolution fusion | flops 2153774592 | bytes 13111296 | tf_op jit(solution)/shard_map/dot_general | solution.py:65
  53.2 5.5 %multiply_convert_fusion = (bf16[512,4096]{1,0:T(8,128)(2,1)}, f32[512]{0:T(512)S(1)}) fusion(f32[512,4096]{1,0:T(8,128)S(1)} %get-tuple-element.17, f32[512]{0:T(512)S(1)} %get-tuple-element.15, f32[512]{0:T(512)S(1)} %get-tuple-element.14, s32[512]{0:T(512)S(1)} %sub.79), kind=kLoop, calls=%fused_computation.11 | loop fusion | flops 18873856 | bytes 12591104 | tf_op jit(solution)/shard_map/convert_element_type | solution.py:77
  58.6 0.8 broadcast_in_dim.95
  59.5 6.0 %all-to-all-start.2 = ((f32[64,1,1024]{2,1,0:T(1,128)}), f32[64,1,1024]{2,1,0:T(1,128)S(1)}, u32[]{:S(2)}, u32[]{:S(2)}) async-start(f32[64,1,1024]{2,1,0:T(1,128)} %broadcast_in_dim.95), calls=%async_computation.2 | async-start | bytes 524288 | tf_op jit(solution)/shard_map/all_to_all | solution.py:17
  65.5 4.7 %gather_fusion = bf16[512,512]{1,0:T(8,128)(2,1)S(1)} fusion(bf16[4096,512]{1,0:T(8,128)(2,1)} %fusion.2, s32[1024]{0:T(1024)S(1)} %pad_clamp_fusion), kind=kCustom, calls=%fused_computation | custom fusion | bytes 1050624 | tf_op jit(solution)/shard_map/jit(_take)/gather | solution.py:87
  70.2 7.0 %all-to-all-done.2 = f32[64,1,1024]{2,1,0:T(1,128)S(1)} async-done(((f32[64,1,1024]{2,1,0:T(1,128)}), f32[64,1,1024]{2,1,0:T(1,128)S(1)}, u32[]{:S(2)}, u32[]{:S(2)}) %all-to-all-start.2) | async-done | bytes 262176 | tf_op jit(solution)/shard_map/all_to_all | solution.py:17
  77.2 0.2 reduce_sum.80
  77.4 6.6 %fusion.10 = bf16[64,8,512]{2,1,0:T(8,128)(2,1)} fusion(bf16[512,4096]{1,0:T(8,128)(2,1)} %get-tuple-element.7, bf16[4096,512]{1,0:T(8,128)(2,1)} %fusion.2, bf16[512,512]{1,0:T(8,128)(2,1)S(1)} %gather_fusion, f32[512]{0:T(512)S(1)} %get-tuple-element.4, f32[512]{0:T(512)S(1)} %get-tuple-element.10, pred[512]{0:T(512)(128)(4,1)S(1)} %compare_and_fusion), kind=kOutput, calls=%fused_computation.21 | convolution fusion | flops 2149056512 | bytes 9441792 | tf_op jit(solution)/shard_map/dot_general | solution.py:86
  84.0 5.7 %all-to-all-start.3 = ((bf16[64,8,512]{2,1,0:T(8,128)(2,1)}), bf16[64,8,512]{2,1,0:T(8,128)(2,1)S(1)}, u32[]{:S(2)}, u32[]{:S(2)}) async-start(bf16[64,8,512]{2,1,0:T(8,128)(2,1)} %fusion.10), calls=%async_computation.3 | async-start | bytes 1048576 | tf_op jit(solution)/shard_map/all_to_all | solution.py:53
  89.7 8.0 %fusion.13 = f32[4096,512]{1,0:T(8,128)} fusion(bf16[512,4096]{1,0:T(8,128)(2,1)} %get-tuple-element.7, bf16[64,8,512]{2,1,0:T(8,128)(2,1)S(1)} %all-to-all-done.1, f32[512]{0:T(512)S(1)} %get-tuple-element.10), kind=kOutput, calls=%fused_computation.25 | convolution fusion | flops 2148270080 | bytes 13109248 | tf_op jit(solution)/shard_map/dot_general | solution.py:94
  97.8 10.4 %scatter_custom_fusion = f32[4096,512]{1,0:T(8,128)} fusion(f32[4096,512]{1,0:T(8,128)} %fusion.13, s32[512]{0:T(512)S(1)} %bitcast.24, bf16[64,8,512]{2,1,0:T(8,128)(2,1)S(1)} %all-to-all-done.1, f32[512]{0:T(512)S(1)} %get-tuple-element.3), kind=kCustom, calls=%fused_computation.23 | custom fusion | flops 786432 | bytes 8914944 | tf_op jit(solution)/shard_map/scatter-add | solution.py:99
  108.2 0.0 copy-start
  108.2 0.0 copy-start.1
  108.2 6.3 %fusion.3 = f32[4096]{0:T(1024)S(1)} fusion(f32[4096,512]{1,0:T(8,128)} %scatter_custom_fusion, bf16[4096,512]{1,0:T(8,128)(2,1)} %param.5, f32[4096]{0:T(1024)S(1)} %add_rsqrt_fusion), kind=kLoop, calls=%fused_computation.7 | loop fusion | flops 8384512 | bytes 12615680 | tf_op jit(solution)/shard_map/reduce_sum | solution.py:138
  114.5 0.6 dynamic-slice_subtract_fusion
  115.1 0.0 copy-done
  115.1 1.4 %copy-done.1 = f32[4096,512]{1,0:T(8,128)S(1)} copy-done((f32[4096,512]{1,0:T(8,128)S(1)}, f32[4096,512]{1,0:T(8,128)}, u32[]{:S(2)}) %copy-start.1) | copy-done | bytes 8388632
  116.5 0.0 copy-start.2
  116.5 4.6 %fusion.5 = f32[4096,512]{1,0:T(8,128)} fusion(f32[4096,512]{1,0:T(8,128)S(1)} %copy-done.1, bf16[4096,512]{1,0:T(8,128)(2,1)S(1)} %copy-done, f32[4096]{0:T(1024)S(1)} %fusion.3, f32[4096]{0:T(1024)S(1)} %add_rsqrt_fusion), kind=kLoop, calls=%fused_computation.9 | loop fusion | flops 10485760 | bytes 21004288 | tf_op jit(solution)/shard_map/mul | solution.py:137
  121.2 0.0 all-to-all-done.3
  121.2 0.1 convert_reduce_fusion
  121.3 0.0 copy-done.2
  121.3 0.2 fusion.24
  121.5 0.7 fusion.26
  (8 shorter events, 0.1 us)
Async XLA Ops:
  1.9 23.0 %all-to-all-start = ((s32[64,1,8]{2,1,0:T(1,128)}), s32[64,1,8]{2,1,0:T(1,128)S(1)}, u32[]{:S(2)}, u32[]{:S(2)}) async-start(s32[64,1,8]{2,1,0:T(1,128)} %broadcast_in_dim.56), calls=%async_computation | async-start | bytes 65536 | tf_op jit(solution)/shard_map/all_to_all | solution.py:17
  25.7 22.8 %all-to-all-start.1 = ((bf16[64,8,512]{2,1,0:T(8,128)(2,1)}), bf16[64,8,512]{2,1,0:T(8,128)(2,1)S(1)}, u32[]{:S(2)}, u32[]{:S(2)}) async-start(bf16[64,8,512]{2,1,0:T(8,128)(2,1)} %broadcast_in_dim.57), calls=%async_computation.1 | async-start | bytes 1048576 | tf_op jit(solution)/shard_map/all_to_all | solution.py:17
  59.5 17.7 %all-to-all-start.2 = ((f32[64,1,1024]{2,1,0:T(1,128)}), f32[64,1,1024]{2,1,0:T(1,128)S(1)}, u32[]{:S(2)}, u32[]{:S(2)}) async-start(f32[64,1,1024]{2,1,0:T(1,128)} %broadcast_in_dim.95), calls=%async_computation.2 | async-start | bytes 524288 | tf_op jit(solution)/shard_map/all_to_all | solution.py:17
  84.0 37.2 %all-to-all-start.3 = ((bf16[64,8,512]{2,1,0:T(8,128)(2,1)}), bf16[64,8,512]{2,1,0:T(8,128)(2,1)S(1)}, u32[]{:S(2)}, u32[]{:S(2)}) async-start(bf16[64,8,512]{2,1,0:T(8,128)(2,1)} %fusion.10), calls=%async_computation.3 | async-start | bytes 1048576 | tf_op jit(solution)/shard_map/all_to_all | solution.py:53
  108.2 6.9 %copy-start = (bf16[4096,512]{1,0:T(8,128)(2,1)S(1)}, bf16[4096,512]{1,0:T(8,128)(2,1)}, u32[]{:S(2)}) copy-start(bf16[4096,512]{1,0:T(8,128)(2,1)} %param.5) | copy-start | bytes 12582916
  108.2 8.3 %copy-start.1 = (f32[4096,512]{1,0:T(8,128)S(1)}, f32[4096,512]{1,0:T(8,128)}, u32[]{:S(2)}) copy-start(f32[4096,512]{1,0:T(8,128)} %scatter_custom_fusion) | copy-start | bytes 25165828
  116.5 4.8 %copy-start.2 = (bf16[8,512]{1,0:T(8,128)(2,1)S(1)}, bf16[8,512]{1,0:T(8,128)(2,1)}, u32[]{:S(2)}) copy-start(bf16[8,512]{1,0:T(8,128)(2,1)} %param.3) | copy-start | bytes 24580
where the time goes:
time: 123 us; the launch traced here: 122 us
  other arithmetic  38.1 us (31%)
  starting transfers between devices  30 us (24%)
  waiting for transfers between devices  24.2 us (20%)
  matrix products  19.3 us (16%)
  local copies, waits for them, and re-layouts  9.77 us (8%)
    all_to_all x3, starting transfers between devices, from_everyone(): lax.all_to_all(jnp.broadcast_to(shard[None], (peers, *shard.shape)), axis...  24.2 us
    all_to_all x3, waiting for transfers between devices, from_everyone(): lax.all_to_all(jnp.broadcast_to(shard[None], (peers, *shard.shape)), axis...  24.2 us
    scatter-add x1, other arithmetic, class_term(): return product.at[drop_index].add(updates, mode='drop')  10.4 us
    dot_general x1, matrix products, class_term(): lax.dot_general(weighted, scaled, (((0,), (0,)), ((), ())), preferred_ele...  8.04 us
    dot_general x1, matrix products, row_term(): jnp.dot(weighted, center_block, preferred_element_type=jnp.float32)  6.59 us
    reduce_sum x1, other arithmetic, per_device(): jnp.sum(units_w * grad_hat_w, axis=1, keepdims=True)  6.28 us
    all_to_all x1, starting transfers between devices, sum_at_owner(): lax.all_to_all(blocks, axis, split_axis=0, concat_axis=0, tiled=True)  5.75 us
    convert_element_type x1, other arithmetic, score_block(): (logit_scale * exp_terms * jnp.where(target_mask, slopes[:, None], 1.0))....  5.47 us
  transfers between devices with their start and end apart: 4, of which 3 were waited for; matrix products, arithmetic and copies ran while one was open for 37% of the time, Pallas kernels for 0%

commit v1 on v0

v1 whole, which is shorter than its diff:
```python
import math

import jax
import jax.numpy as jnp
from jax import lax
from jax.experimental import pallas as pl
from jax.experimental.pallas import tpu as pltpu
from jax.sharding import PartitionSpec as P

logit_scale = 64.0
margin_cosine = math.cos(0.5)
margin_sine = math.sin(0.5)
sine_soften = 0.04
norm_eps = 1e-06

slope2 = logit_scale * math.log2(math.e)
shift2 = slope2 - math.log2(logit_scale)

LANES = 128
MIB = 1024 * 1024
f32, bf16, i32 = jnp.float32, jnp.bfloat16, jnp.int32
VMEM = pl.BlockSpec(memory_space=pltpu.VMEM)
SMEM = pl.BlockSpec(memory_space=pltpu.SMEM)


def params(mib):
    return pltpu.CompilerParams(vmem_limit_bytes=mib * MIB)


def cost(flops, nbytes):
    return pl.CostEstimate(flops=int(flops), bytes_accessed=int(nbytes), transcendentals=0)


def dot(a, b, ca, cb):
    return lax.dot_general(a, b, (((ca,), (cb,)), ((), ())), preferred_element_type=f32)


def norm_kernel(c_ref, o_ref):
    w = c_ref[...].astype(f32)
    inv = lax.rsqrt(jnp.sum(w * w, axis=1, keepdims=True) + norm_eps)
    o_ref[...] = (w * inv).astype(bf16)


def unit_centers(centers, tile=1024):
    n, d = centers.shape
    return pl.pallas_call(
        norm_kernel,
        grid=(n // tile,),
        in_specs=[pl.BlockSpec((tile, d), lambda i: (i, 0))],
        out_specs=pl.BlockSpec((tile, d), lambda i: (i, 0)),
        out_shape=jax.ShapeDtypeStruct((n, d), bf16),
        compiler_params=params(16),
        cost_estimate=cost(3e9, 8 * MIB),
        name="unit_centers",
    )(centers)


def digit_weights(shape, dim):
    lane = lax.broadcasted_iota(i32, shape, dim)
    return jnp.where(lane == 0, 4096.0, jnp.where(lane == 1, 64.0, jnp.where(lane == 2, 1.0, 0.0)))


def score_kernel(base_ref, g_ref, c_ref, w_ref, e_ref, st_ref, pay_ref, *, tile, peers):
    n, d = c_ref.shape
    m = g_ref.shape[0]
    x = g_ref[:, :d].astype(f32)
    inv = lax.rsqrt(jnp.sum(x * x, axis=1, keepdims=True) + norm_eps)
    e_ref[...] = (x * inv).astype(bf16)
    weights = digit_weights((8, LANES), 1).astype(bf16)
    lab = dot(weights, g_ref[:, d:], 1, 1).astype(i32) - base_ref[0]
    lab1 = lab[0:1, :]
    ehat = e_ref[...]

    def step(k, carry):
        tot, tcs = carry
        row0 = pl.multiple_of(k * tile, tile)
        cos = dot(c_ref[pl.ds(row0, tile), :], ehat, 1, 1)
        row = lax.broadcasted_iota(i32, (tile, m), 0) + row0
        hit = row == lab1
        e = jnp.where(hit, 0.0, jnp.exp2(cos * slope2 - shift2))
        w_ref[pl.ds(row0, tile), :] = e.astype(bf16)
        tot = tot + e.reshape(tile // 8, 8, m).sum(axis=0)
        tcs = tcs + jnp.where(hit, cos, 0.0).reshape(tile // 8, 8, m).sum(axis=0)
        return tot, tcs

    zero = jnp.zeros((8, m), f32)
    tot, tcs = lax.fori_loop(0, n // tile, step, (zero, zero))
    tot = tot.sum(axis=0, keepdims=True)
    tc = tcs.sum(axis=0, keepdims=True)
    owned = (lab1 >= 0) & (lab1 < n)
    sine = jnp.sqrt(1.0 + sine_soften - tc * tc)
    shifted = tc * margin_cosine - sine * margin_sine
    slopes = jnp.where(owned, margin_cosine + margin_sine * tc / sine, 0.0)
    texp = jnp.where(owned, jnp.exp2(slope2 * shifted - shift2), 0.0)
    total = (tot + texp) * (1.0 / logit_scale)
    target = jnp.where(owned, logit_scale * shifted, 0.0)
    row8 = lax.broadcasted_iota(i32, (8, m), 0)
    st_ref[...] = jnp.where(row8 == 0, slopes, jnp.where(row8 == 1, texp, lab.astype(f32)))
    per = LANES // (m // peers)
    for p in range(peers):
        q = p // per
        pay_ref[p] = jnp.concatenate([total, target[:, q * LANES : (q + 1) * LANES]], axis=1)


def scores(base, gathered, chat, peers):
    n, d = chat.shape
    m = gathered.shape[0]
    return pl.pallas_call(
        lambda *refs: score_kernel(*refs, tile=256, peers=peers),
        in_specs=[SMEM, VMEM, VMEM],
        out_specs=[VMEM, VMEM, VMEM, VMEM],
        out_shape=[
            jax.ShapeDtypeStruct((n, m), bf16),
            jax.ShapeDtypeStruct((m, d), bf16),
            jax.ShapeDtypeStruct((8, m), f32),
            jax.ShapeDtypeStruct((peers, 1, m + LANES), f32),
        ],
        compiler_params=params(24),
        cost_estimate=cost(4e9, 8 * MIB),
        name="scores",
    )(base, gathered, chat)


def rows_kernel(st_ref, w_ref, c_ref, p_ref, t_ref, *, tile):
    n, d = c_ref.shape
    m = p_ref.shape[0]
    lab1 = st_ref[2:3, :].astype(i32)

    def step(k, _):
        row0 = pl.multiple_of(k * tile, tile)
        c = c_ref[pl.ds(row0, tile), :]
        row = lax.broadcasted_iota(i32, (tile, m), 0) + row0
        hot = jnp.where(row == lab1, 1.0, 0.0).astype(bf16)
        prod = dot(w_ref[pl.ds(row0, tile), :], c, 0, 0)
        pick = dot(hot, c, 0, 0)

        @pl.when(k == 0)
        def _():
            p_ref[...] = prod
            t_ref[...] = pick

        @pl.when(k > 0)
        def _():
            p_ref[...] += prod
            t_ref[...] += pick

        return 0

    lax.fori_loop(0, n // tile, step, 0)


def row_sums(stats, weighted, chat):
    n, d = chat.shape
    m = weighted.shape[1]
    return pl.pallas_call(
        lambda *refs: rows_kernel(*refs, tile=1024),
        in_specs=[VMEM, VMEM, VMEM],
        out_specs=[VMEM, VMEM],
        out_shape=[jax.ShapeDtypeStruct((m, d), f32), jax.ShapeDtypeStruct((m, d), f32)],
        compiler_params=params(24),
        cost_estimate=cost(6e9, 10 * MIB),
        name="row_sums",
    )(stats, weighted, chat)


def close_kernel(tr_ref, st_ref, p_ref, t_ref, q_ref, col_ref, tot_ref):
    m = p_ref.shape[0]
    sums = tr_ref[...].sum(axis=0)
    tot_ref[...] = sums
    total = sums[:, :m]
    coef = st_ref[0:1, :] * (st_ref[1:2, :] / total - logit_scale)
    row = lax.broadcasted_iota(i32, (LANES, m), 0)
    cols = jnp.where(row == 0, 1.0 / total, coef).T
    col_ref[...] = cols
    q_ref[...] = (p_ref[...] * cols[:, 0:1] + t_ref[...] * cols[:, 1:2]).astype(bf16)


def close_rows(received, stats, prod, pick):
    m, d = prod.shape
    return pl.pallas_call(
        close_kernel,
        in_specs=[VMEM, VMEM, VMEM, VMEM],
        out_specs=[VMEM, VMEM, VMEM],
        out_shape=[
            jax.ShapeDtypeStruct((m, d), bf16),
            jax.ShapeDtypeStruct((m, LANES), f32),
            jax.ShapeDtypeStruct((1, m + LANES), f32),
        ],
        compiler_params=params(16),
        cost_estimate=cost(1e9, 3 * MIB),
        name="close_rows",
    )(received, stats, prod, pick)


def class_kernel(st_ref, e_ref, col_ref, w_ref, c_ref, o_ref, s_ref, hi_ref, lo_ref, *, tile):
    m = e_ref.shape[0]

    @pl.when(pl.program_id(0) == 0)
    def _():
        e = e_ref[...].astype(f32)
        s_ref[...] = (e * col_ref[:, 0:1]).astype(bf16)
        own = e * col_ref[:, 1:2]
        hi = own.astype(bf16)
        hi_ref[...] = hi
        lo_ref[...] = (own - hi.astype(f32)).astype(bf16)

    row0 = pl.program_id(0) * tile
    lab1 = st_ref[2:3, :].astype(i32)
    row = lax.broadcasted_iota(i32, (tile, m), 0) + row0
    hot = jnp.where(row == lab1, 1.0, 0.0).astype(bf16)
    grad = dot(w_ref[...], s_ref[...], 1, 0)
    grad = grad + dot(hot, hi_ref[...], 1, 0)
    grad = grad + dot(hot, lo_ref[...], 1, 0)
    w = c_ref[...].astype(f32)
    inv = lax.rsqrt(jnp.sum(w * w, axis=1, keepdims=True) + norm_eps)
    units = w * inv
    along = jnp.sum(units * grad, axis=1, keepdims=True)
    o_ref[...] = inv * (grad - units * along)


def class_grads(stats, ehat, cols, weighted, centers, tile=512):
    n, d = centers.shape
    m = ehat.shape[0]
    whole = lambda a: pl.BlockSpec(a.shape, lambda i: (0, 0))
    return pl.pallas_call(
        lambda *refs: class_kernel(*refs, tile=tile),
        grid=(n // tile,),
        in_specs=[
            whole(stats),
            whole(ehat),
            whole(cols),
            pl.BlockSpec((tile, m), lambda i: (i, 0)),
            pl.BlockSpec((tile, d), lambda i: (i, 0)),
        ],
        out_specs=pl.BlockSpec((tile, d), lambda i: (i, 0)),
        out_shape=jax.ShapeDtypeStruct((n, d), f32),
        scratch_shapes=[pltpu.VMEM((m, d), bf16)] * 3,
        compiler_params=params(24),
        cost_estimate=cost(8e9, 16 * MIB),
        name="class_grads",
    )(stats, ehat, cols, weighted, centers)


def final_kernel(x_ref, r_ref, o_ref):
    x = x_ref[...].astype(f32)
    inv = lax.rsqrt(jnp.sum(x * x, axis=1, keepdims=True) + norm_eps)
    units = x * inv
    grad = r_ref[...].astype(f32).sum(axis=0)
    o_ref[...] = inv * (grad - units * jnp.sum(units * grad, axis=1, keepdims=True))


def example_grads(embeddings, received):
    return pl.pallas_call(
        final_kernel,
        in_specs=[VMEM, VMEM],
        out_specs=VMEM,
        out_shape=jax.ShapeDtypeStruct(embeddings.shape, f32),
        compiler_params=params(8),
        cost_estimate=cost(1e7, MIB),
        name="example_grads",
    )(embeddings, received)


def exchange(blocks):
    return lax.all_to_all(blocks, "cls", 0, 0, tiled=True)


def per_device(embeddings, labels, centers):
    own, d = embeddings.shape
    n = centers.shape[0]
    peers = lax.axis_size("cls")
    m = own * peers
    index = lax.axis_index("cls")
    lane = lax.broadcasted_iota(i32, (own, LANES), 1)
    lab = labels[:, None]
    digits = jnp.where(
        lane == 0, lab >> 12, jnp.where(lane == 1, (lab >> 6) & 63, jnp.where(lane == 2, lab & 63, 0))
    )
    packed = jnp.concatenate([embeddings, digits.astype(bf16)], axis=1)
    gathered = exchange(jnp.broadcast_to(packed[None], (peers, own, d + LANES)))
    chat = unit_centers(centers)
    base = (index * n).astype(i32)[None]
    weighted, ehat, stats, pay = scores(base, gathered.reshape(m, d + LANES), chat, peers)
    received = exchange(pay)
    prod, pick = row_sums(stats, weighted, chat)
    rows, cols, sums = close_rows(received, stats, prod, pick)
    rows = exchange(rows.reshape(peers, own, d))
    center_grad = class_grads(stats, ehat, cols, weighted, centers)
    per = LANES // own
    own_total = lax.dynamic_slice(sums[0], (index * own,), (own,))
    own_target = lax.dynamic_slice(sums[0], (m + (index % per) * own,), (own,))
    losses = jnp.log(own_total) + logit_scale - own_target
    emb_grad = example_grads(embeddings, rows)
    return (losses, emb_grad, center_grad)


def solution(mesh):
    in_specs = (P(("dp", "cls"), None), P(("dp", "cls")), P(("dp", "cls"), None))
    out_specs = (P(("dp", "cls")), P(("dp", "cls"), None), P(("dp", "cls"), None))
    return jax.shard_map(
        per_device, mesh=mesh, in_specs=in_specs, out_specs=out_specs, check_vma=False
    )
```

time: 123 us -> 94.9 us (0.77)
  other arithmetic: 38.1 us -> 2.04 us
  Pallas kernels: 0 us -> 27.4 us
  matrix products: 19.3 us -> 0 us
  local copies, waits for them, and re-layouts: 9.77 us -> 18 us
  waiting for transfers between devices: 24.2 us -> 16.8 us
    pallas_call x0 -> x6, Pallas kernels: none -> 27.4 us  [the longest x1 10.3 us: class_grads(): pl.pallas_call(lambda *refs: class_kernel(*refs, tile=tile), grid=(n // t...]
    dot_general x3 -> x0, matrix products: 19.3 us -> none  [the longest x1 8.04 us: class_term(): lax.dot_general(weighted, scaled, (((0,), (0,)), ((), ())), preferred_ele...]
    unnamed x6 -> x18, local copies, waits for them, and re-layouts: 1.43 us -> 17.1 us
    reduce_sum x6 -> x0, other arithmetic: 10.7 us -> none  [the longest x1 6.28 us: per_device(): jnp.sum(units_w * grad_hat_w, axis=1, keepdims=True)]
    scatter-add x1 -> x0, other arithmetic: 10.4 us -> none  [class_term(): return product.at[drop_index].add(updates, mode='drop')]
    convert_element_type x3 -> x1, other arithmetic: 10.3 us -> 0.08 us  [per_device(): packed = jnp.concatenate([embeddings, digits.astype(bf16)], axis=1)]
    all_to_all x4 -> x3, waiting for transfers between devices: 24.2 us -> 16.8 us  [exchange(): return lax.all_to_all(blocks, 'cls', 0, 0, tiled=True)]
    mul x2 -> x0, other arithmetic: 5.33 us -> none  [the longest x1 4.64 us: per_device(): inv_w * (grad_hat_w - units_w * jnp.sum(units_w * grad_hat_w, axis=1, kee...]
  transfers between devices with their start and end apart: 4 -> 3, of which waited for: 3 -> 3; matrix products, arithmetic and copies ran while one was open for 37% -> 1% of each run, Pallas kernels for 0% -> 19%
where the time goes in v1:
time: 94.9 us; the launch traced here: 94.3 us
  starting transfers between devices  29.3 us (31%)
  Pallas kernels  27.4 us (29%)
  local copies, waits for them, and re-layouts  18 us (19%)
  waiting for transfers between devices  16.8 us (18%)
  other arithmetic  2.04 us (2%)
    all_to_all x3, starting transfers between devices, exchange(): return lax.all_to_all(blocks, 'cls', 0, 0, tiled=True)  29.3 us
    unnamed x18, local copies, waits for them, and re-layouts  17.1 us
    all_to_all x3, waiting for transfers between devices, exchange(): return lax.all_to_all(blocks, 'cls', 0, 0, tiled=True)  16.8 us
    pallas_call x1, Pallas kernels, class_grads(): pl.pallas_call(lambda *refs: class_kernel(*refs, tile=tile), grid=(n // t...  10.3 us
    pallas_call x1, Pallas kernels, scores(): pl.pallas_call(lambda *refs: score_kernel(*refs, tile=256, peers=peers),...  7.8 us
    pallas_call x1, Pallas kernels, row_sums(): pl.pallas_call(lambda *refs: rows_kernel(*refs, tile=1024), in_specs=[VME...  5.87 us
  transfers between devices with their start and end apart: 3, of which 3 were waited for; matrix products, arithmetic and copies ran while one was open for 1% of the time, Pallas kernels for 19%

profile of v1, /device:TPU:16, one launch (start us, length us, event | category | flops | bytes accessed | tf_op | source)
XLA Modules:
  0.0 94.3 jit_solution(834859865109411604)
XLA Ops:
  0.7 0.7 broadcast_shift-right-arithmetic_fusion
  1.3 0.1 select_convert_fusion
  1.4 0.7 pad_maximum_fusion
  2.1 0.9 broadcast_in_dim.37
  3.0 12.7 %all-to-all-start = ((bf16[64,8,640]{2,1,0:T(8,128)(2,1)}), bf16[64,8,640]{2,1,0:T(8,128)(2,1)S(1)}, u32[]{:S(2)}, u32[]{:S(2)}) async-start(bf16[64,8,640]{2,1,0:T(8,128)(2,1)} %broadcast_in_dim.37), calls=%async_computation | async-start | bytes 1310720 | tf_op jit(solution)/shard_map/all_to_all | solution.py:265
  15.7 0.0 copy-start.1
  15.7 2.2 %copy-done.1 = bf16[4096,512]{1,0:T(8,128)(2,1)S(1)} copy-done((bf16[4096,512]{1,0:T(8,128)(2,1)S(1)}, bf16[4096,512]{1,0:T(8,128)(2,1)}, u32[]{:S(2)}) %copy-start.1) | copy-done | bytes 4194328
  17.9 1.4 %unit_centers.1.refs_2_ = bf16[4096,512]{1,0:T(8,128)(2,1)S(1)} custom-call(bf16[4096,512]{1,0:T(8,128)(2,1)S(1)} %copy-done.1), custom_call_target="tpu_custom_call" | custom-call | flops 3000000000 | bytes 8388608 | tf_op jit(solution)/shard_map/unit_centers/pallas_call | solution.py:46
  19.2 0.0 copy-start.3
  19.3 2.0 %copy-done.3 = bf16[4096,512]{1,0:T(8,128)(2,1)} copy-done((bf16[4096,512]{1,0:T(8,128)(2,1)}, bf16[4096,512]{1,0:T(8,128)(2,1)S(1)}, u32[]{:S(2)}) %copy-start.3) | copy-done | bytes 4194328
  21.3 14.9 %all-to-all-done = bf16[64,8,640]{2,1,0:T(8,128)(2,1)S(1)} async-done(((bf16[64,8,640]{2,1,0:T(8,128)(2,1)}), bf16[64,8,640]{2,1,0:T(8,128)(2,1)S(1)}, u32[]{:S(2)}, u32[]{:S(2)}) %all-to-all-start) | async-done | bytes 655392 | tf_op jit(solution)/shard_map/all_to_all | solution.py:265
  36.2 0.0 copy-start.4
  36.2 2.2 %copy-done.4 = bf16[4096,512]{1,0:T(8,128)(2,1)S(1)} copy-done((bf16[4096,512]{1,0:T(8,128)(2,1)S(1)}, bf16[4096,512]{1,0:T(8,128)(2,1)}, u32[]{:S(2)}) %copy-start.4) | copy-done | bytes 4194328
  38.3 7.8 %scores.1 = (bf16[4096,512]{1,0:T(8,128)(2,1)S(1)}, bf16[512,512]{1,0:T(8,128)(2,1)S(1)}, f32[8,512]{1,0:T(8,128)S(1)}, f32[64,1,640]{2,1,0:T(1,128)}) custom-call(s32[1]{0:T(128)} %bitcast.refs_0_, bf16[512,640]{1,0:T(8,128)(2,1)S(1)} %bitcast.5, bf16[4096,512]{1,0:T(8,128)(2,1)S(1)} %copy-done.4), custom_call_target="tpu_custom_call" | custom-call | flops 4000000000 | bytes 8388608 | tf_op jit(solution)/shard_map/scores/pallas_call | solution.py:108
  46.2 0.0 copy-start.6
  46.2 2.0 %copy-done.6 = bf16[4096,512]{1,0:T(8,128)(2,1)} copy-done((bf16[4096,512]{1,0:T(8,128)(2,1)}, bf16[4096,512]{1,0:T(8,128)(2,1)S(1)}, u32[]{:S(2)}) %copy-start.6) | copy-done | bytes 4194328
  48.1 6.0 %all-to-all-start.1 = ((f32[64,1,640]{2,1,0:T(1,128)}), f32[64,1,640]{2,1,0:T(1,128)S(1)}, u32[]{:S(2)}, u32[]{:S(2)}) async-start(f32[64,1,640]{2,1,0:T(1,128)} %get-tuple-element.12), calls=%async_computation.1 | async-start | bytes 327680 | tf_op jit(solution)/shard_map/all_to_all | solution.py:265
  54.1 0.0 copy-start.5
  54.1 2.2 %copy-done.5 = bf16[4096,512]{1,0:T(8,128)(2,1)S(1)} copy-done((bf16[4096,512]{1,0:T(8,128)(2,1)S(1)}, bf16[4096,512]{1,0:T(8,128)(2,1)}, u32[]{:S(2)}) %copy-start.5) | copy-done | bytes 4194328
  56.3 0.0 copy-start.7
  56.3 2.2 %copy-done.7 = bf16[4096,512]{1,0:T(8,128)(2,1)S(1)} copy-done((bf16[4096,512]{1,0:T(8,128)(2,1)S(1)}, bf16[4096,512]{1,0:T(8,128)(2,1)}, u32[]{:S(2)}) %copy-start.7) | copy-done | bytes 4194328
  58.5 5.9 %row_sums.1 = (f32[512,512]{1,0:T(8,128)S(1)}, f32[512,512]{1,0:T(8,128)S(1)}) custom-call(f32[8,512]{1,0:T(8,128)S(1)} %get-tuple-element.13.refs_0_.st_ref, bf16[4096,512]{1,0:T(8,128)(2,1)S(1)} %copy-done.7, bf16[4096,512]{1,0:T(8,128)(2,1)S(1)} %copy-done.5), custom_call_target="tpu_custom_call" | custom-call | flops 6000000000 | bytes 10485760 | tf_op jit(solution)/shard_map/row_sums/pallas_call | solution.py:155
  64.3 0.5 all-to-all-done.1.tr_ref
  64.9 1.3 %close_rows.1 = (bf16[512,512]{1,0:T(8,128)(2,1)}, f32[512,128]{1,0:T(8,128)S(1)}, f32[1,640]{1,0:T(1,128)S(1)}) custom-call(f32[64,1,640]{2,1,0:T(1,128)S(1)} %all-to-all-done.1.tr_ref, f32[8,512]{1,0:T(8,128)S(1)} %get-tuple-element.13.refs_0_.st_ref, f32[512,512]{1,0:T(8,128)S(1)} %get-tuple-element.15.p_ref, f32[512,512]{1,0:T(8,128)S(1)} %get-tuple-element.16.t_ref), custom_call_target="tpu_custom_call" | custom-call | flops 1000000000 | bytes 3145728 | tf_op jit(solution)/shard_map/close_rows/pallas_call | solution.py:180
  66.1 10.7 %all-to-all-start.2 = ((bf16[64,8,512]{2,1,0:T(8,128)(2,1)}), bf16[64,8,512]{2,1,0:T(8,128)(2,1)S(1)}, u32[]{:S(2)}, u32[]{:S(2)}) async-start(bf16[64,8,512]{2,1,0:T(8,128)(2,1)} %bitcast.3), calls=%async_computation.2 | async-start | bytes 1048576 | tf_op jit(solution)/shard_map/all_to_all | solution.py:265
  76.9 0.6 subtract_bitcast_fusion
  77.5 0.0 copy-start.2
  77.5 2.2 %copy-done.2 = bf16[4096,512]{1,0:T(8,128)(2,1)S(1)} copy-done((bf16[4096,512]{1,0:T(8,128)(2,1)S(1)}, bf16[4096,512]{1,0:T(8,128)(2,1)}, u32[]{:S(2)}) %copy-start.2) | copy-done | bytes 4194328
  79.6 0.0 copy-start.8
  79.6 2.2 %copy-done.8 = bf16[4096,512]{1,0:T(8,128)(2,1)S(1)} copy-done((bf16[4096,512]{1,0:T(8,128)(2,1)S(1)}, bf16[4096,512]{1,0:T(8,128)(2,1)}, u32[]{:S(2)}) %copy-start.8) | copy-done | bytes 4194328
  81.8 0.0 copy-start
  81.8 10.3 %class_grads.1 = f32[4096,512]{1,0:T(8,128)} custom-call(f32[8,512]{1,0:T(8,128)S(1)} %get-tuple-element.13.refs_0_.st_ref, bf16[512,512]{1,0:T(8,128)(2,1)S(1)} %get-tuple-element.19.refs_1_, f32[512,128]{1,0:T(8,128)S(1)} %get-tuple-element.20.refs_2_, bf16[4096,512]{1,0:T(8,128)(2,1)S(1)} %copy-done.8, bf16[4096,512]{1,0:T(8,128)(2,1)S(1)} %copy-done.2), custom_call_target="tpu_custom_call" | custom-call | flops 8000000000 | bytes 16777216 | tf_op jit(solution)/shard_map/class_grads/pallas_call | solution.py:225
  92.2 1.4 %all-to-all-done.2.r_ref = bf16[64,8,512]{2,1,0:T(8,128)(2,1)S(1)} async-done(((bf16[64,8,512]{2,1,0:T(8,128)(2,1)}), bf16[64,8,512]{2,1,0:T(8,128)(2,1)S(1)}, u32[]{:S(2)}, u32[]{:S(2)}) %all-to-all-start.2) | async-done | bytes 524320 | tf_op jit(solution)/shard_map/all_to_all | solution.py:265
  93.6 0.0 copy-done
  93.6 0.8 example_grads.1
  (2 shorter events, 0.0 us)
Async XLA Ops:
  3.0 33.2 %all-to-all-start = ((bf16[64,8,640]{2,1,0:T(8,128)(2,1)}), bf16[64,8,640]{2,1,0:T(8,128)(2,1)S(1)}, u32[]{:S(2)}, u32[]{:S(2)}) async-start(bf16[64,8,640]{2,1,0:T(8,128)(2,1)} %broadcast_in_dim.37), calls=%async_computation | async-start | bytes 1310720 | tf_op jit(solution)/shard_map/all_to_all | solution.py:265
  15.7 2.2 %copy-start.1 = (bf16[4096,512]{1,0:T(8,128)(2,1)S(1)}, bf16[4096,512]{1,0:T(8,128)(2,1)}, u32[]{:S(2)}) copy-start(bf16[4096,512]{1,0:T(8,128)(2,1)} %refs_4_.1) | copy-start | bytes 12582916
  19.2 2.0 %copy-start.3 = (bf16[4096,512]{1,0:T(8,128)(2,1)}, bf16[4096,512]{1,0:T(8,128)(2,1)S(1)}, u32[]{:S(2)}) copy-start(bf16[4096,512]{1,0:T(8,128)(2,1)S(1)} %unit_centers.1.refs_2_) | copy-start | bytes 12582916
  36.2 2.2 %copy-start.4 = (bf16[4096,512]{1,0:T(8,128)(2,1)S(1)}, bf16[4096,512]{1,0:T(8,128)(2,1)}, u32[]{:S(2)}) copy-start(bf16[4096,512]{1,0:T(8,128)(2,1)} %copy-done.3) | copy-start | bytes 12582916
  46.2 2.0 %copy-start.6 = (bf16[4096,512]{1,0:T(8,128)(2,1)}, bf16[4096,512]{1,0:T(8,128)(2,1)S(1)}, u32[]{:S(2)}) copy-start(bf16[4096,512]{1,0:T(8,128)(2,1)S(1)} %get-tuple-element.14.refs_1_.refs_3_) | copy-start | bytes 12582916
  48.1 16.8 %all-to-all-start.1 = ((f32[64,1,640]{2,1,0:T(1,128)}), f32[64,1,640]{2,1,0:T(1,128)S(1)}, u32[]{:S(2)}, u32[]{:S(2)}) async-start(f32[64,1,640]{2,1,0:T(1,128)} %get-tuple-element.12), calls=%async_computation.1 | async-start | bytes 327680 | tf_op jit(solution)/shard_map/all_to_all | solution.py:265
  54.1 2.2 %copy-start.5 = (bf16[4096,512]{1,0:T(8,128)(2,1)S(1)}, bf16[4096,512]{1,0:T(8,128)(2,1)}, u32[]{:S(2)}) copy-start(bf16[4096,512]{1,0:T(8,128)(2,1)} %copy-done.3) | copy-start | bytes 12582916
  56.3 2.2 %copy-start.7 = (bf16[4096,512]{1,0:T(8,128)(2,1)S(1)}, bf16[4096,512]{1,0:T(8,128)(2,1)}, u32[]{:S(2)}) copy-start(bf16[4096,512]{1,0:T(8,128)(2,1)} %copy-done.6) | copy-start | bytes 12582916
  66.1 27.4 %all-to-all-start.2 = ((bf16[64,8,512]{2,1,0:T(8,128)(2,1)}), bf16[64,8,512]{2,1,0:T(8,128)(2,1)S(1)}, u32[]{:S(2)}, u32[]{:S(2)}) async-start(bf16[64,8,512]{2,1,0:T(8,128)(2,1)} %bitcast.3), calls=%async_computation.2 | async-start | bytes 1048576 | tf_op jit(solution)/shard_map/all_to_all | solution.py:265
  77.5 2.2 %copy-start.2 = (bf16[4096,512]{1,0:T(8,128)(2,1)S(1)}, bf16[4096,512]{1,0:T(8,128)(2,1)}, u32[]{:S(2)}) copy-start(bf16[4096,512]{1,0:T(8,128)(2,1)} %refs_4_.1) | copy-start | bytes 12582916
  79.6 2.2 %copy-start.8 = (bf16[4096,512]{1,0:T(8,128)(2,1)S(1)}, bf16[4096,512]{1,0:T(8,128)(2,1)}, u32[]{:S(2)}) copy-start(bf16[4096,512]{1,0:T(8,128)(2,1)} %copy-done.6) | copy-start | bytes 12582916
  81.8 11.7 %copy-start = (bf16[8,512]{1,0:T(8,128)(2,1)S(1)}, bf16[8,512]{1,0:T(8,128)(2,1)}, u32[]{:S(2)}) copy-start(bf16[8,512]{1,0:T(8,128)(2,1)} %x_ref.1) | copy-start | bytes 24580

commit v2 on v0

v2 whole, which is shorter than its diff:
```python
import functools
import math

import jax
import jax.numpy as jnp
from jax import lax
from jax.experimental import pallas as pl
from jax.experimental.pallas import tpu as pltpu
from jax.sharding import Mesh
from jax.sharding import PartitionSpec as P

logit_scale = 64.0
margin_cosine = math.cos(0.5)
margin_sine = math.sin(0.5)
sine_soften = 0.04
norm_eps = 1e-06

slope2 = logit_scale * math.log2(math.e)
shift2 = slope2 - math.log2(logit_scale)

LANES = 128
MIB = 1024 * 1024
NEAR = ("x", "y")
FAR = "z"
f32, bf16, i32 = jnp.float32, jnp.bfloat16, jnp.int32
VMEM = pl.BlockSpec(memory_space=pltpu.VMEM)
SMEM = pl.BlockSpec(memory_space=pltpu.SMEM)
HBM = pl.BlockSpec(memory_space=pltpu.HBM)


def params(mib):
    return pltpu.CompilerParams(vmem_limit_bytes=mib * MIB)


def dot(a, b, ca, cb):
    return lax.dot_general(a, b, (((ca,), (cb,)), ((), ())), preferred_element_type=f32)


def inverse_norm(x):
    return lax.rsqrt(jnp.sum(x * x, axis=1, keepdims=True) + norm_eps)


def margin(cosine):
    sine = jnp.sqrt(1.0 + sine_soften - cosine * cosine)
    shifted = cosine * margin_cosine - sine * margin_sine
    slope = margin_cosine + margin_sine * cosine / sine
    return jnp.exp2(slope2 * shifted - shift2), logit_scale * shifted, slope


def total_rows(total):
    row8 = lax.broadcasted_iota(i32, (8, total.shape[1]), 0)
    out = jnp.zeros(row8.shape, f32)
    rest = total
    for r in range(3):
        part = rest.astype(bf16).astype(f32)
        out = jnp.where(row8 == r, part, out)
        rest = rest - part
    return out.astype(bf16)


def pack_kernel(x_ref, lab_ref, o_ref):
    rows, d = x_ref.shape
    row = lax.broadcasted_iota(i32, (rows, LANES), 0)
    lane = lax.broadcasted_iota(i32, (rows, LANES), 1)
    lab = jnp.zeros((rows, LANES), i32)
    for j in range(rows):
        lab = jnp.where(row == j, lab_ref[j], lab)
    digit = jnp.where(lane == 0, lab >> 12, jnp.where(lane == 1, (lab >> 6) & 63, lab & 63))
    digit = jnp.where(lane < 3, digit, 0).astype(f32).astype(bf16)
    for p in range(o_ref.shape[0]):
        o_ref[p, :, :d] = x_ref[...]
        o_ref[p, :, d:] = digit


def pack(embeddings, labels, peers):
    rows, d = embeddings.shape
    return pl.pallas_call(
        pack_kernel,
        in_specs=[VMEM, SMEM],
        out_specs=VMEM,
        out_shape=jax.ShapeDtypeStruct((peers, rows, d + LANES), bf16),
        compiler_params=params(4),
        name="pack",
    )(embeddings, labels)


def digit_weights(shape):
    lane = lax.broadcasted_iota(i32, shape, 1)
    return jnp.where(lane == 0, 4096.0, jnp.where(lane == 1, 64.0, jnp.where(lane == 2, 1.0, 0.0)))


def score_kernel(
    base_ref, g_ref, c_hbm, w_hbm, e_ref, st_ref, pay_ref, raw, chat, wv, isem, osem, *, tile, chunk, iblk
):
    n, d = c_hbm.shape
    m = g_ref.shape[0]
    groups = pay_ref.shape[0]
    chunks = n // chunk

    def load(k):
        rows = pl.ds(pl.multiple_of(k * chunk, chunk), chunk)
        return pltpu.make_async_copy(c_hbm.at[rows], raw.at[rows], isem.at[k])

    def save(k):
        rows = pl.ds(pl.multiple_of(k * chunk, chunk), chunk)
        return pltpu.make_async_copy(wv.at[rows], w_hbm.at[rows], osem.at[k])

    for k in range(chunks):
        load(k).start()
    x = g_ref[:, :d].astype(f32)
    e_ref[...] = (x * inverse_norm(x)).astype(bf16)
    tail = g_ref[:, d:]
    lab = dot(digit_weights((8, LANES)).astype(bf16), tail, 1, 1).astype(i32) - base_ref[0]
    lab1 = lab[0:1, :]
    col = jnp.sum(tail.astype(f32) * digit_weights((1, LANES)), axis=1, keepdims=True)
    col = col.astype(i32) - base_ref[0]

    def unit(k):
        rows = pl.ds(pl.multiple_of(k * tile, tile), tile)
        w = raw[rows, :].astype(f32)
        chat[rows, :] = (w * inverse_norm(w)).astype(bf16)

    per = chunk // tile
    load(0).wait()
    unit(0)

    def step(k, carry):
        tot, tcs = carry
        nxt = jnp.minimum(k + 1, n // tile - 1)

        @pl.when((lax.rem(nxt, per) == 0) & (k + 1 < n // tile))
        def _():
            load(nxt // per).wait()

        row0 = pl.multiple_of(k * tile, tile)
        cos = dot(chat[pl.ds(row0, tile), :], e_ref[...], 1, 1)
        unit(nxt)
        row = lax.broadcasted_iota(i32, (tile, m), 0) + row0
        hit = row == lab1
        e = jnp.where(hit, 0.0, jnp.exp2(cos * slope2 - shift2))
        wv[pl.ds(row0, tile), :] = e.astype(bf16)
        tot = tot + e.reshape(tile // 8, 8, m).sum(axis=0)
        tcs = tcs + jnp.where(hit, cos, 0.0).reshape(tile // 8, 8, m).sum(axis=0)

        @pl.when(lax.rem(k, per) == per - 1)
        def _():
            save(k // per).start()

        return tot, tcs

    zero = jnp.zeros((8, m), f32)
    tot, tcs = lax.fori_loop(0, n // tile, step, (zero, zero))
    owned = (lab1 >= 0) & (lab1 < n)
    texp, _, slope = margin(tcs.sum(axis=0, keepdims=True))
    texp = jnp.where(owned, texp, 0.0)
    slope = jnp.where(owned, slope, 0.0)
    total = (tot.sum(axis=0, keepdims=True) + texp) * (1.0 / logit_scale)
    row8 = lax.broadcasted_iota(i32, (8, m), 0)
    st_ref[...] = jnp.where(row8 == 0, slope, jnp.where(row8 == 1, texp, lab.astype(f32)))
    sums = total_rows(total)
    span = m // groups
    for p in range(groups):
        pay_ref[p, 2 * span :, :] = sums
    lane = lax.broadcasted_iota(i32, (iblk, n), 1)
    for b in range(m // iblk):
        rows = slice(b * iblk, (b + 1) * iblk)
        hot = jnp.where(lane == col[rows], 1.0, 0.0).astype(bf16)
        prod = dot(wv[:, rows], chat[...], 0, 0).astype(bf16)
        pick = dot(hot, chat[...], 1, 0).astype(bf16)
        for q in range(iblk // span):
            p = b * (iblk // span) + q
            pay_ref[p, 0:span, :] = prod[q * span : (q + 1) * span]
            pay_ref[p, span : 2 * span, :] = pick[q * span : (q + 1) * span]
    for k in range(chunks):
        save(k).wait()


def scores(base, gathered, centers, groups, tile=512, chunk=512, iblk=128):
    n, d = centers.shape
    m = gathered.shape[0]
    return pl.pallas_call(
        functools.partial(score_kernel, tile=tile, chunk=chunk, iblk=iblk),
        in_specs=[SMEM, VMEM, HBM],
        out_specs=[HBM, VMEM, VMEM, VMEM],
        out_shape=[
            jax.ShapeDtypeStruct((n, m), bf16),
            jax.ShapeDtypeStruct((m, d), bf16),
            jax.ShapeDtypeStruct((8, m), f32),
            jax.ShapeDtypeStruct((groups, 2 * (m // groups) + 8, d), bf16),
        ],
        scratch_shapes=[
            pltpu.VMEM((n, d), bf16),
            pltpu.VMEM((n, d), bf16),
            pltpu.VMEM((n, m), bf16),
            pltpu.SemaphoreType.DMA((n // chunk,)),
            pltpu.SemaphoreType.DMA((n // chunk,)),
        ],
        compiler_params=params(32),
        name="scores",
    )(base, gathered, centers)


def middle_kernel(r_ref, o_ref):
    far, rows, d = o_ref.shape
    own = rows // 3
    half = far * own
    sums = r_ref[...].astype(f32).sum(axis=0)
    low = sums[: 2 * half].astype(bf16)
    totals = total_rows(sums[2 * half :].sum(axis=0, keepdims=True))
    for q in range(far):
        o_ref[q, :own, :] = low[q * own : (q + 1) * own]
        o_ref[q, own : 2 * own, :] = low[half + q * own : half + (q + 1) * own]
        o_ref[q, 2 * own :, :] = totals


def middle(received, far, own):
    d = received.shape[2]
    return pl.pallas_call(
        middle_kernel,
        in_specs=[VMEM],
        out_specs=VMEM,
        out_shape=jax.ShapeDtypeStruct((far, 3 * own, d), bf16),
        compiler_params=params(8),
        name="middle",
    )(received)


def grad_kernel(
    own_ref, r_ref, x_ref, st_ref, e_ref, w_hbm, c_hbm, l_ref, xg_ref, o_hbm, wv, raw, out, wsem, csem, osem, *, chunk
):
    n, d = c_hbm.shape
    m = e_ref.shape[0]
    own = x_ref.shape[0]
    chunks = n // chunk

    def load(k):
        rows = pl.ds(pl.multiple_of(k * chunk, chunk), chunk)
        return (
            pltpu.make_async_copy(w_hbm.at[rows], wv.at[rows], wsem.at[k]),
            pltpu.make_async_copy(c_hbm.at[rows], raw.at[rows], csem.at[k]),
        )

    def save(k):
        rows = pl.ds(pl.multiple_of(k * chunk, chunk), chunk)
        return pltpu.make_async_copy(out.at[rows], o_hbm.at[rows], osem.at[k])

    for k in range(chunks):
        for copy in load(k):
            copy.start()
    sums = r_ref[...].astype(f32).sum(axis=0)
    total = sums[2 * own :].sum(axis=0, keepdims=True)
    scale = 1.0 / total
    coef = st_ref[0:1, :] * (st_ref[1:2, :] * scale - logit_scale)
    lab1 = st_ref[2:3, :].astype(i32)

    def step(k, _):
        for copy in load(k):
            copy.wait()
        rows = pl.ds(pl.multiple_of(k * chunk, chunk), chunk)
        hit = lax.broadcasted_iota(i32, (chunk, m), 0) == lab1 - k * chunk
        share = jnp.where(hit, coef, wv[rows, :].astype(f32) * scale).astype(bf16)
        grad = dot(share, e_ref[...], 1, 0)
        w = raw[rows, :].astype(f32)
        inv = inverse_norm(w)
        along = jnp.sum(w * grad, axis=1, keepdims=True) * (inv * inv)
        out[rows, :] = inv * (grad - w * along)
        save(k).start()
        return 0

    lax.fori_loop(0, chunks, step, 0)

    x = x_ref[...].astype(f32)
    inv = inverse_norm(x)
    units = x * inv
    unit16 = units.astype(bf16).astype(f32)
    pick = sums[own : 2 * own]
    texp, logit, slope = margin(jnp.sum(unit16 * pick, axis=1, keepdims=True))
    lane = lax.broadcasted_iota(i32, (own, m), 1)
    row = lax.broadcasted_iota(i32, (own, m), 0)
    own_total = jnp.sum(jnp.where(lane == row + own_ref[0], total, 0.0), axis=1, keepdims=True)
    grad = sums[:own] / own_total + (slope * (texp / own_total - logit_scale)) * pick
    xg_ref[...] = inv * (grad - units * jnp.sum(units * grad, axis=1, keepdims=True))
    loss = jnp.log(own_total) + logit_scale - logit
    spread = jnp.where(lane[:, :LANES] == row[:, :LANES], loss, 0.0).sum(axis=0, keepdims=True)
    l_ref[...] = spread[:, :own]
    for k in range(chunks):
        save(k).wait()


def grads(own_first, received, embeddings, stats, ehat, weighted, centers, chunk=512):
    n, d = centers.shape
    m = ehat.shape[0]
    own = embeddings.shape[0]
    return pl.pallas_call(
        functools.partial(grad_kernel, chunk=chunk),
        in_specs=[SMEM, VMEM, VMEM, VMEM, VMEM, HBM, HBM],
        out_specs=[VMEM, VMEM, HBM],
        out_shape=[
            jax.ShapeDtypeStruct((1, own), f32),
            jax.ShapeDtypeStruct((own, d), f32),
            jax.ShapeDtypeStruct((n, d), f32),
        ],
        scratch_shapes=[
            pltpu.VMEM((n, m), bf16),
            pltpu.VMEM((n, d), bf16),
            pltpu.VMEM((n, d), f32),
            pltpu.SemaphoreType.DMA((n // chunk,)),
            pltpu.SemaphoreType.DMA((n // chunk,)),
            pltpu.SemaphoreType.DMA((n // chunk,)),
        ],
        compiler_params=params(32),
        name="grads",
    )(own_first, received, embeddings, stats, ehat, weighted, centers)


def exchange(blocks, axis):
    return lax.all_to_all(blocks, axis, 0, 0, tiled=True)


def per_device(embeddings, labels, centers):
    own, d = embeddings.shape
    n = centers.shape[0]
    far = lax.axis_size(FAR)
    near = lax.axis_size(NEAR)
    m = own * far * near
    at_near = lax.axis_index(NEAR)
    at_far = lax.axis_index(FAR)
    place = lax.axis_index(("x", FAR, "y"))
    base = (place * n).astype(i32)[None]
    own_first = ((at_near * far + at_far) * own).astype(i32)[None]
    embeddings, base, own_first = lax.optimization_barrier((embeddings, base, own_first))
    line = exchange(pack(embeddings, labels, far), FAR).reshape(1, far * own, d + LANES)
    gathered = exchange(jnp.broadcast_to(line, (near, *line.shape[1:])), NEAR)
    weighted, ehat, stats, pay = scores(base, gathered.reshape(m, d + LANES), centers, near)
    half = middle(exchange(pay, NEAR), far, own)
    losses, emb_grad, center_grad = grads(
        own_first, exchange(half, FAR), embeddings, stats, ehat, weighted, centers
    )
    return (losses.reshape(own), emb_grad, center_grad)


def solution(mesh):
    dp = mesh.shape["dp"]
    fine = Mesh(mesh.devices.reshape(4, mesh.shape["cls"] // 8, 2, dp), ("x", FAR, "y", "dp"))
    rows = ("dp", "x", FAR, "y")
    in_specs = (P(rows, None), P(rows), P(rows, None))
    out_specs = (P(rows), P(rows, None), P(rows, None))
    return jax.shard_map(
        per_device, mesh=fine, in_specs=in_specs, out_specs=out_specs, check_vma=False
    )
```

time: 123 us -> 84.5 us (0.69)
  blocking collectives: 0 us -> 60.4 us
  other arithmetic: 38.1 us -> 0 us
  starting transfers between devices: 30 us -> 0 us
  waiting for transfers between devices: 24.2 us -> 0 us
  Pallas kernels: 0 us -> 19.5 us
  matrix products: 19.3 us -> 0 us
  local copies, waits for them, and re-layouts: 9.77 us -> 3.59 us
    all_to_all x0 -> x4, blocking collectives: none -> 60.4 us  [exchange(): return lax.all_to_all(blocks, axis, 0, 0, tiled=True)]
    all_to_all x4 -> x0, starting transfers between devices: 30 us -> none  [the longest x3 24.2 us: from_everyone(): lax.all_to_all(jnp.broadcast_to(shard[None], (peers, *shard.shape)), axis...]
    all_to_all x4 -> x0, waiting for transfers between devices: 24.2 us -> none  [the longest x3 24.2 us: from_everyone(): lax.all_to_all(jnp.broadcast_to(shard[None], (peers, *shard.shape)), axis...]
    pallas_call x0 -> x4, Pallas kernels: none -> 19.5 us  [the longest x1 11.7 us: scores(): pl.pallas_call(functools.partial(score_kernel, tile=tile, chunk=chunk, ib...]
    dot_general x3 -> x0, matrix products: 19.3 us -> none  [the longest x1 8.04 us: class_term(): lax.dot_general(weighted, scaled, (((0,), (0,)), ((), ())), preferred_ele...]
    reduce_sum x6 -> x0, other arithmetic: 10.7 us -> none  [the longest x1 6.28 us: per_device(): jnp.sum(units_w * grad_hat_w, axis=1, keepdims=True)]
    scatter-add x1 -> x0, other arithmetic: 10.4 us -> none  [class_term(): return product.at[drop_index].add(updates, mode='drop')]
    convert_element_type x3 -> x0, other arithmetic: 10.3 us -> none  [the longest x1 5.47 us: score_block(): (logit_scale * exp_terms * jnp.where(target_mask, slopes[:, None], 1.0))....]
  transfers between devices with their start and end apart: 4 -> 0, of which waited for: 3 -> 0; matrix products, arithmetic and copies ran while one was open for 37% -> 0% of each run, Pallas kernels for 0% -> 0%
where the time goes in v2:
time: 84.5 us; the launch traced here: 84.2 us
  blocking collectives  60.4 us (71%)
  Pallas kernels  19.5 us (23%)
  local copies, waits for them, and re-layouts  3.59 us (4%)
    all_to_all x4, blocking collectives, exchange(): return lax.all_to_all(blocks, axis, 0, 0, tiled=True)  60.4 us
    pallas_call x1, Pallas kernels, scores(): pl.pallas_call(functools.partial(score_kernel, tile=tile, chunk=chunk, ib...  11.7 us
    pallas_call x1, Pallas kernels, grads(): pl.pallas_call(functools.partial(grad_kernel, chunk=chunk), in_specs=[SME...  7.1 us
    unnamed x10, local copies, waits for them, and re-layouts  3.54 us

profile of v2, /device:TPU:16, one launch (start us, length us, event | category | flops | bytes accessed | tf_op | source)
XLA Modules:
  0.0 84.2 jit_solution(14293862620641559213)
XLA Ops:
  0.6 0.0 copy-start.2
  0.7 0.7 copy-done.2
  1.3 0.0 copy-start.4
  1.3 0.7 copy-done.4
  2.0 0.6 pack.1
  2.6 16.8 %all_to_all.20 = bf16[8,8,640]{2,1,0:T(8,128)(2,1)S(1)} all-to-all(bf16[8,8,640]{2,1,0:T(8,128)(2,1)S(1)} %pack.1), channel_id=1, replica_groups=mesh['x'=4,'z'=8,'y'=2,'dp'=4] {'z'}, dimensions={0} | all-to-all | bytes 163840 | tf_op jit(solution)/shard_map/all_to_all | solution.py:317
  19.4 0.1 broadcast_in_dim.16
  19.4 14.8 %all_to_all.21 = bf16[8,64,640]{2,1,0:T(8,128)(2,1)S(1)} all-to-all(bf16[8,64,640]{2,1,0:T(8,128)(2,1)S(1)} %broadcast_in_dim.16), channel_id=1, replica_groups=mesh['x'=4,'z'=8,'y'=2,'dp'=4] {'x','y'}, dimensions={0} | all-to-all | bytes 1310720 | tf_op jit(solution)/shard_map/all_to_all | solution.py:317
  34.2 0.0 copy-start
  34.2 2.2 %copy-done = bf16[4096,512]{1,0:T(8,128)(2,1)S(1)} copy-done((bf16[4096,512]{1,0:T(8,128)(2,1)S(1)}, bf16[4096,512]{1,0:T(8,128)(2,1)}, u32[]{:S(2)}) %copy-start) | copy-done | bytes 4194328
  36.4 0.0 copy-start.1
  36.4 0.0 copy-start.3
  36.4 11.7 %scores.1 = (bf16[4096,512]{1,0:T(8,128)(2,1)S(1)}, bf16[512,512]{1,0:T(8,128)(2,1)S(1)}, f32[8,512]{1,0:T(8,128)S(1)}, bf16[8,136,512]{2,1,0:T(8,128)(2,1)S(1)}) custom-call(s32[1]{0:T(128)} %bitcast.base_ref, bf16[512,640]{1,0:T(8,128)(2,1)S(1)} %bitcast.5, bf16[4096,512]{1,0:T(8,128)(2,1)S(1)} %copy-done), custom_call_target="tpu_custom_call" | custom-call | tf_op jit(solution)/shard_map/scores/pallas_call | solution.py:181
  48.1 16.6 %all_to_all.22.r_ref = bf16[8,136,512]{2,1,0:T(8,128)(2,1)S(1)} all-to-all(bf16[8,136,512]{2,1,0:T(8,128)(2,1)S(1)} %get-tuple-element.16), channel_id=1, replica_groups=mesh['x'=4,'z'=8,'y'=2,'dp'=4] {'x','y'}, dimensions={0} | all-to-all | bytes 2228224 | tf_op jit(solution)/shard_map/all_to_all | solution.py:317
  64.7 0.2 middle.1
  64.9 12.2 %all_to_all.23.r_ref = bf16[8,24,512]{2,1,0:T(8,128)(2,1)S(1)} all-to-all(bf16[8,24,512]{2,1,0:T(8,128)(2,1)S(1)} %middle.1), channel_id=1, replica_groups=mesh['x'=4,'z'=8,'y'=2,'dp'=4] {'z'}, dimensions={0} | all-to-all | bytes 393216 | tf_op jit(solution)/shard_map/all_to_all | solution.py:317
  77.1 0.0 copy-done.1
  77.1 0.0 copy-done.3
  77.1 7.1 %grads.1 = (f32[1,8]{1,0:T(1,128)}, f32[8,512]{1,0:T(8,128)}, f32[4096,512]{1,0:T(8,128)}) custom-call(s32[1]{0:T(128)} %bitcast.1.own_ref, bf16[8,24,512]{2,1,0:T(8,128)(2,1)S(1)} %all_to_all.23.r_ref, bf16[8,512]{1,0:T(8,128)(2,1)S(1)} %copy-done.3, f32[8,512]{1,0:T(8,128)S(1)} %get-tuple-element.17.st_ref, bf16[512,512]{1,0:T(8,128)(2,1)S(1)} %get-tuple-element.18.e_ref, ...), custom_call_target="tpu_custom_call" | custom-call | tf_op jit(solution)/shard_map/grads/pallas_call | solution.py:294
Async XLA Ops:
  0.6 0.7 copy-start.2
  1.3 0.7 copy-start.4
  34.2 2.2 %copy-start = (bf16[4096,512]{1,0:T(8,128)(2,1)S(1)}, bf16[4096,512]{1,0:T(8,128)(2,1)}, u32[]{:S(2)}) copy-start(bf16[4096,512]{1,0:T(8,128)(2,1)} %c_hbm.3) | copy-start | bytes 12582916
  36.4 40.6 %copy-start.1 = (bf16[4096,512]{1,0:T(8,128)(2,1)S(1)}, bf16[4096,512]{1,0:T(8,128)(2,1)}, u32[]{:S(2)}) copy-start(bf16[4096,512]{1,0:T(8,128)(2,1)} %c_hbm.3) | copy-start | bytes 12582916
  36.4 40.6 %copy-start.3 = (bf16[8,512]{1,0:T(8,128)(2,1)S(1)}, bf16[8,512]{1,0:T(8,128)(2,1)}, u32[]{:S(2)}) copy-start(bf16[8,512]{1,0:T(8,128)(2,1)} %x_ref.1) | copy-start | bytes 24580

commit v3 on v2

--- a/solution.py
+++ b/solution.py
@@ -30,6 +30,10 @@
 
 def params(mib):
     return pltpu.CompilerParams(vmem_limit_bytes=mib * MIB)
+
+
+def in_hbm(x):
+    return pltpu.with_memory_space_constraint(x, pltpu.HBM)
 
 
 def dot(a, b, ca, cb):
@@ -58,8 +62,16 @@
     return out.astype(bf16)
 
 
-def pack_kernel(x_ref, lab_ref, o_ref):
+def pack_kernel(x_hbm, lab_hbm, o_ref, x_ref, lab_ref, sem):
     rows, d = x_ref.shape
+    copies = (
+        pltpu.make_async_copy(lab_hbm, lab_ref, sem.at[0]),
+        pltpu.make_async_copy(x_hbm, x_ref, sem.at[1]),
+    )
+    for copy in copies:
+        copy.start()
+    for copy in copies:
+        copy.wait()
     row = lax.broadcasted_iota(i32, (rows, LANES), 0)
     lane = lax.broadcasted_iota(i32, (rows, LANES), 1)
     lab = jnp.zeros((rows, LANES), i32)
@@ -76,12 +88,17 @@
     rows, d = embeddings.shape
     return pl.pallas_call(
         pack_kernel,
-        in_specs=[VMEM, SMEM],
+        in_specs=[HBM, HBM],
         out_specs=VMEM,
         out_shape=jax.ShapeDtypeStruct((peers, rows, d + LANES), bf16),
+        scratch_shapes=[
+            pltpu.VMEM((rows, d), bf16),
+            pltpu.SMEM((rows,), i32),
+            pltpu.SemaphoreType.DMA((2,)),
+        ],
         compiler_params=params(4),
         name="pack",
-    )(embeddings, labels)
+    )(in_hbm(embeddings), in_hbm(labels))
 
 
 def digit_weights(shape):
@@ -90,7 +107,7 @@
 
 
 def score_kernel(
-    base_ref, g_ref, c_hbm, w_hbm, e_ref, st_ref, pay_ref, raw, chat, wv, isem, osem, *, tile, chunk, iblk
+    base_ref, g_ref, c_hbm, wv, raw, e_ref, st_ref, pay_ref, chat, isem, *, tile, chunk, iblk
 ):
     n, d = c_hbm.shape
     m = g_ref.shape[0]
@@ -100,10 +117,6 @@
     def load(k):
         rows = pl.ds(pl.multiple_of(k * chunk, chunk), chunk)
         return pltpu.make_async_copy(c_hbm.at[rows], raw.at[rows], isem.at[k])
-
-    def save(k):
-        rows = pl.ds(pl.multiple_of(k * chunk, chunk), chunk)
-        return pltpu.make_async_copy(wv.at[rows], w_hbm.at[rows], osem.at[k])
 
     for k in range(chunks):
         load(k).start()
@@ -141,11 +154,6 @@
         wv[pl.ds(row0, tile), :] = e.astype(bf16)
         tot = tot + e.reshape(tile // 8, 8, m).sum(axis=0)
         tcs = tcs + jnp.where(hit, cos, 0.0).reshape(tile // 8, 8, m).sum(axis=0)
-
-        @pl.when(lax.rem(k, per) == per - 1)
-        def _():
-            save(k // per).start()
-
         return tot, tcs
 
     zero = jnp.zeros((8, m), f32)
@@ -171,8 +179,6 @@
             p = b * (iblk // span) + q
             pay_ref[p, 0:span, :] = prod[q * span : (q + 1) * span]
             pay_ref[p, span : 2 * span, :] = pick[q * span : (q + 1) * span]
-    for k in range(chunks):
-        save(k).wait()
 
 
 def scores(base, gathered, centers, groups, tile=512, chunk=512, iblk=128):
@@ -181,23 +187,21 @@
     return pl.pallas_call(
         functools.partial(score_kernel, tile=tile, chunk=chunk, iblk=iblk),
         in_specs=[SMEM, VMEM, HBM],
-        out_specs=[HBM, VMEM, VMEM, VMEM],
+        out_specs=[VMEM] * 5,
         out_shape=[
-            jax.ShapeDtypeStruct((n, m), bf16),
+            pltpu.VMEM((n, m), bf16),
+            pltpu.VMEM((n, d), bf16),
             jax.ShapeDtypeStruct((m, d), bf16),
             jax.ShapeDtypeStruct((8, m), f32),
             jax.ShapeDtypeStruct((groups, 2 * (m // groups) + 8, d), bf16),
         ],
         scratch_shapes=[
             pltpu.VMEM((n, d), bf16),
-            pltpu.VMEM((n, d), bf16),
-            pltpu.VMEM((n, m), bf16),
             pltpu.SemaphoreType.DMA((n // chunk,)),
-            pltpu.SemaphoreType.DMA((n // chunk,)),
-        ],
-        compiler_params=params(32),
+        ],
+        compiler_params=params(24),
         name="scores",
-    )(base, gathered, centers)
+    )(base, gathered, in_hbm(centers))
 
 
 def middle_kernel(r_ref, o_ref):
@@ -226,27 +230,17 @@
 
 
 def grad_kernel(
-    own_ref, r_ref, x_ref, st_ref, e_ref, w_hbm, c_hbm, l_ref, xg_ref, o_hbm, wv, raw, out, wsem, csem, osem, *, chunk
+    own_ref, r_ref, x_ref, st_ref, e_ref, wv, raw, l_ref, xg_ref, o_hbm, out, osem, *, chunk
 ):
-    n, d = c_hbm.shape
+    n, d = raw.shape
     m = e_ref.shape[0]
     own = x_ref.shape[0]
     chunks = n // chunk
 
-    def load(k):
-        rows = pl.ds(pl.multiple_of(k * chunk, chunk), chunk)
-        return (
-            pltpu.make_async_copy(w_hbm.at[rows], wv.at[rows], wsem.at[k]),
-            pltpu.make_async_copy(c_hbm.at[rows], raw.at[rows], csem.at[k]),
-        )
-
     def save(k):
         rows = pl.ds(pl.multiple_of(k * chunk, chunk), chunk)
         return pltpu.make_async_copy(out.at[rows], o_hbm.at[rows], osem.at[k])
 
-    for k in range(chunks):
-        for copy in load(k):
-            copy.start()
     sums = r_ref[...].astype(f32).sum(axis=0)
     total = sums[2 * own :].sum(axis=0, keepdims=True)
     scale = 1.0 / total
@@ -254,8 +248,6 @@
     lab1 = st_ref[2:3, :].astype(i32)
 
     def step(k, _):
-        for copy in load(k):
-            copy.wait()
         rows = pl.ds(pl.multiple_of(k * chunk, chunk), chunk)
         hit = lax.broadcasted_iota(i32, (chunk, m), 0) == lab1 - k * chunk
         share = jnp.where(hit, coef, wv[rows, :].astype(f32) * scale).astype(bf16)
@@ -293,7 +285,7 @@
     own = embeddings.shape[0]
     return pl.pallas_call(
         functools.partial(grad_kernel, chunk=chunk),
-        in_specs=[SMEM, VMEM, VMEM, VMEM, VMEM, HBM, HBM],
+        in_specs=[SMEM] + [VMEM] * 6,
         out_specs=[VMEM, VMEM, HBM],
         out_shape=[
             jax.ShapeDtypeStruct((1, own), f32),
@@ -301,14 +293,10 @@
             jax.ShapeDtypeStruct((n, d), f32),
         ],
         scratch_shapes=[
-            pltpu.VMEM((n, m), bf16),
-            pltpu.VMEM((n, d), bf16),
             pltpu.VMEM((n, d), f32),
             pltpu.SemaphoreType.DMA((n // chunk,)),
-            pltpu.SemaphoreType.DMA((n // chunk,)),
-            pltpu.SemaphoreType.DMA((n // chunk,)),
-        ],
-        compiler_params=params(32),
+        ],
+        compiler_params=params(24),
         name="grads",
     )(own_first, received, embeddings, stats, ehat, weighted, centers)
 
@@ -331,10 +319,10 @@
     embeddings, base, own_first = lax.optimization_barrier((embeddings, base, own_first))
     line = exchange(pack(embeddings, labels, far), FAR).reshape(1, far * own, d + LANES)
     gathered = exchange(jnp.broadcast_to(line, (near, *line.shape[1:])), NEAR)
-    weighted, ehat, stats, pay = scores(base, gathered.reshape(m, d + LANES), centers, near)
+    weighted, raw, ehat, stats, pay = scores(base, gathered.reshape(m, d + LANES), centers, near)
     half = middle(exchange(pay, NEAR), far, own)
     losses, emb_grad, center_grad = grads(
-        own_first, exchange(half, FAR), embeddings, stats, ehat, weighted, centers
+        own_first, exchange(half, FAR), embeddings, stats, ehat, weighted, raw
     )
     return (losses.reshape(own), emb_grad, center_grad)
 

time: 84.5 us -> 80.6 us (0.954)
  local copies, waits for them, and re-layouts: 3.59 us -> 0.06 us
    unnamed x10 -> x2, local copies, waits for them, and re-layouts: 3.54 us -> 0.01 us
where the time goes in v3:
time: 80.6 us; the launch traced here: 80.3 us
  blocking collectives  60.5 us (75%)
  Pallas kernels  19.1 us (24%)
    all_to_all x4, blocking collectives, exchange(): return lax.all_to_all(blocks, axis, 0, 0, tiled=True)  60.5 us
    pallas_call x1, Pallas kernels, scores(): pl.pallas_call(functools.partial(score_kernel, tile=tile, chunk=chunk, ib...  11.9 us
    pallas_call x1, Pallas kernels, grads(): pl.pallas_call(functools.partial(grad_kernel, chunk=chunk), in_specs=[SME...  6.38 us

profile of v3, /device:TPU:16, one launch (start us, length us, event | category | flops | bytes accessed | tf_op | source)
XLA Modules:
  0.0 80.3 jit_solution(12865422306922595711)
XLA Ops:
  0.6 0.7 pack.1
  1.4 16.8 %all_to_all.20 = bf16[8,8,640]{2,1,0:T(8,128)(2,1)S(1)} all-to-all(bf16[8,8,640]{2,1,0:T(8,128)(2,1)S(1)} %pack.1), channel_id=1, replica_groups=mesh['x'=4,'z'=8,'y'=2,'dp'=4] {'z'}, dimensions={0} | all-to-all | bytes 163840 | tf_op jit(solution)/shard_map/all_to_all | solution.py:305
  18.2 0.1 broadcast_in_dim.16
  18.3 14.8 %all_to_all.21 = bf16[8,64,640]{2,1,0:T(8,128)(2,1)S(1)} all-to-all(bf16[8,64,640]{2,1,0:T(8,128)(2,1)S(1)} %broadcast_in_dim.16), channel_id=1, replica_groups=mesh['x'=4,'z'=8,'y'=2,'dp'=4] {'x','y'}, dimensions={0} | all-to-all | bytes 1310720 | tf_op jit(solution)/shard_map/all_to_all | solution.py:305
  33.1 0.0 copy-start
  33.1 11.9 %scores.1 = (bf16[4096,512]{1,0:T(8,128)(2,1)S(1)}, bf16[4096,512]{1,0:T(8,128)(2,1)S(1)}, bf16[512,512]{1,0:T(8,128)(2,1)S(1)}, f32[8,512]{1,0:T(8,128)S(1)}, bf16[8,136,512]{2,1,0:T(8,128)(2,1)S(1)}) custom-call(s32[1]{0:T(128)} %bitcast.base_ref, bf16[512,640]{1,0:T(8,128)(2,1)S(1)} %bitcast.5, bf16[4096,512]{1,0:T(8,128)(2,1)} %c_hbm.1), custom_call_target="tpu_custom_call" | custom-call | tf_op jit(solution)/shard_map/scores/pallas_call | solution.py:187
  44.9 16.7 %all_to_all.22.r_ref = bf16[8,136,512]{2,1,0:T(8,128)(2,1)S(1)} all-to-all(bf16[8,136,512]{2,1,0:T(8,128)(2,1)S(1)} %get-tuple-element.17), channel_id=1, replica_groups=mesh['x'=4,'z'=8,'y'=2,'dp'=4] {'x','y'}, dimensions={0} | all-to-all | bytes 2228224 | tf_op jit(solution)/shard_map/all_to_all | solution.py:305
  61.6 0.2 middle.1
  61.8 12.2 %all_to_all.23.r_ref = bf16[8,24,512]{2,1,0:T(8,128)(2,1)S(1)} all-to-all(bf16[8,24,512]{2,1,0:T(8,128)(2,1)S(1)} %middle.1), channel_id=1, replica_groups=mesh['x'=4,'z'=8,'y'=2,'dp'=4] {'z'}, dimensions={0} | all-to-all | bytes 393216 | tf_op jit(solution)/shard_map/all_to_all | solution.py:305
  73.9 0.0 copy-done
  73.9 6.4 %grads.1 = (f32[1,8]{1,0:T(1,128)}, f32[8,512]{1,0:T(8,128)}, f32[4096,512]{1,0:T(8,128)}) custom-call(s32[1]{0:T(128)} %bitcast.1.own_ref, bf16[8,24,512]{2,1,0:T(8,128)(2,1)S(1)} %all_to_all.23.r_ref, bf16[8,512]{1,0:T(8,128)(2,1)S(1)} %copy-done, f32[8,512]{1,0:T(8,128)S(1)} %get-tuple-element.18.st_ref, bf16[512,512]{1,0:T(8,128)(2,1)S(1)} %get-tuple-element.19.e_ref, ...), custom_call_target="tpu_custom_call" | custom-call | tf_op jit(solution)/shard_map/grads/pallas_call | solution.py:286
Async XLA Ops:
  33.1 40.9 %copy-start = (bf16[8,512]{1,0:T(8,128)(2,1)S(1)}, bf16[8,512]{1,0:T(8,128)(2,1)}, u32[]{:S(2)}) copy-start(bf16[8,512]{1,0:T(8,128)(2,1)} %x_ref) | copy-start | bytes 24580

commit v4 on v3

--- a/solution.py
+++ b/solution.py
@@ -106,20 +106,10 @@
     return jnp.where(lane == 0, 4096.0, jnp.where(lane == 1, 64.0, jnp.where(lane == 2, 1.0, 0.0)))
 
 
-def score_kernel(
-    base_ref, g_ref, c_hbm, wv, raw, e_ref, st_ref, pay_ref, chat, isem, *, tile, chunk, iblk
-):
-    n, d = c_hbm.shape
+def score_half(base_ref, g_ref, chat, raw, fetch, w_ref, e_ref, st_ref, acc, pck, *, tile):
+    n, d = chat.shape
     m = g_ref.shape[0]
-    groups = pay_ref.shape[0]
-    chunks = n // chunk
-
-    def load(k):
-        rows = pl.ds(pl.multiple_of(k * chunk, chunk), chunk)
-        return pltpu.make_async_copy(c_hbm.at[rows], raw.at[rows], isem.at[k])
-
-    for k in range(chunks):
-        load(k).start()
+    steps = n // tile
     x = g_ref[:, :d].astype(f32)
     e_ref[...] = (x * inverse_norm(x)).astype(bf16)
     tail = g_ref[:, d:]
@@ -128,80 +118,151 @@
     col = jnp.sum(tail.astype(f32) * digit_weights((1, LANES)), axis=1, keepdims=True)
     col = col.astype(i32) - base_ref[0]
 
+    def span(k):
+        return pl.ds(pl.multiple_of(k * tile, tile), tile)
+
     def unit(k):
-        rows = pl.ds(pl.multiple_of(k * tile, tile), tile)
-        w = raw[rows, :].astype(f32)
-        chat[rows, :] = (w * inverse_norm(w)).astype(bf16)
-
-    per = chunk // tile
-    load(0).wait()
-    unit(0)
-
-    def step(k, carry):
-        tot, tcs = carry
-        nxt = jnp.minimum(k + 1, n // tile - 1)
-
-        @pl.when((lax.rem(nxt, per) == 0) & (k + 1 < n // tile))
-        def _():
-            load(nxt // per).wait()
-
-        row0 = pl.multiple_of(k * tile, tile)
-        cos = dot(chat[pl.ds(row0, tile), :], e_ref[...], 1, 1)
-        unit(nxt)
-        row = lax.broadcasted_iota(i32, (tile, m), 0) + row0
-        hit = row == lab1
+        w = raw[span(k), :].astype(f32)
+        chat[span(k), :] = (w * inverse_norm(w)).astype(bf16)
+
+    def score(k, tot, tcs):
+        cos = dot(chat[span(k), :], e_ref[...], 1, 1)
+        hit = lax.broadcasted_iota(i32, (tile, m), 0) == lab1 - k * tile
         e = jnp.where(hit, 0.0, jnp.exp2(cos * slope2 - shift2))
-        wv[pl.ds(row0, tile), :] = e.astype(bf16)
+        w_ref[span(k), :] = e.astype(bf16)
         tot = tot + e.reshape(tile // 8, 8, m).sum(axis=0)
         tcs = tcs + jnp.where(hit, cos, 0.0).reshape(tile // 8, 8, m).sum(axis=0)
         return tot, tcs
 
+    def gather(k):
+        hot = lax.broadcasted_iota(i32, (m, tile), 1) == col - k * tile
+        c = chat[span(k), :]
+        prod = dot(w_ref[span(k), :], c, 0, 0)
+        pick = dot(jnp.where(hot, 1.0, 0.0).astype(bf16), c, 1, 0)
+        return prod, pick
+
     zero = jnp.zeros((8, m), f32)
-    tot, tcs = lax.fori_loop(0, n // tile, step, (zero, zero))
+    if raw is not None:
+        fetch(0).wait()
+        unit(0)
+        fetch(1).wait()
+        unit(1)
+    tot, tcs = score(0, zero, zero)
+    acc[...] = jnp.zeros(acc.shape, f32)
+    pck[...] = jnp.zeros(pck.shape, f32)
+
+    def step(k, carry):
+        tot, tcs = carry
+        if raw is not None:
+            ahead = jnp.minimum(k + 1, steps - 1)
+
+            @pl.when(k + 1 < steps)
+            def _():
+                fetch(ahead).wait()
+
+        prod, pick = gather(k - 1)
+        tot, tcs = score(k, tot, tcs)
+        if raw is not None:
+            unit(ahead)
+        acc[...] += prod
+        pck[...] += pick
+        return tot, tcs
+
+    tot, tcs = lax.fori_loop(1, steps, step, (tot, tcs))
+    prod, pick = gather(steps - 1)
+    acc[...] += prod
+    pck[...] += pick
     owned = (lab1 >= 0) & (lab1 < n)
     texp, _, slope = margin(tcs.sum(axis=0, keepdims=True))
     texp = jnp.where(owned, texp, 0.0)
     slope = jnp.where(owned, slope, 0.0)
     total = (tot.sum(axis=0, keepdims=True) + texp) * (1.0 / logit_scale)
     row8 = lax.broadcasted_iota(i32, (8, m), 0)
-    st_ref[...] = jnp.where(row8 == 0, slope, jnp.where(row8 == 1, texp, lab.astype(f32)))
-    sums = total_rows(total)
-    span = m // groups
-    for p in range(groups):
-        pay_ref[p, 2 * span :, :] = sums
-    lane = lax.broadcasted_iota(i32, (iblk, n), 1)
-    for b in range(m // iblk):
-        rows = slice(b * iblk, (b + 1) * iblk)
-        hot = jnp.where(lane == col[rows], 1.0, 0.0).astype(bf16)
-        prod = dot(wv[:, rows], chat[...], 0, 0).astype(bf16)
-        pick = dot(hot, chat[...], 1, 0).astype(bf16)
-        for q in range(iblk // span):
-            p = b * (iblk // span) + q
-            pay_ref[p, 0:span, :] = prod[q * span : (q + 1) * span]
-            pay_ref[p, span : 2 * span, :] = pick[q * span : (q + 1) * span]
-
-
-def scores(base, gathered, centers, groups, tile=512, chunk=512, iblk=128):
+    tail = jnp.where(row8 == 3, total, lab.astype(f32))
+    st_ref[...] = jnp.where(row8 == 0, slope, jnp.where(row8 == 1, texp, tail))
+    return total
+
+
+def first_kernel(base_ref, g_ref, c_hbm, w_ref, raw, chat, e_ref, st_ref, pay_ref, acc, pck, sem, *, tile):
+    n = c_hbm.shape[0]
+
+    def fetch(k):
+        rows = pl.ds(pl.multiple_of(k * tile, tile), tile)
+        return pltpu.make_async_copy(c_hbm.at[rows], raw.at[rows], sem.at[k])
+
+    for k in range(n // tile):
+        fetch(k).start()
+    score_half(base_ref, g_ref, chat, raw, fetch, w_ref, e_ref, st_ref, acc, pck, tile=tile)
+    blocks, rows = pay_ref.shape[0], pay_ref.shape[1] // 2
+    for p in range(blocks):
+        pay_ref[p, :rows, :] = acc[p * rows : (p + 1) * rows].astype(bf16)
+        pay_ref[p, rows:, :] = pck[p * rows : (p + 1) * rows].astype(bf16)
+
+
+def second_kernel(
+    base_ref, side_ref, g_ref, chat, first_ref, firstst_ref, w_ref, e_ref, st_ref, pay_ref, acc, pck, *, tile
+):
+    m = g_ref.shape[0]
+    total = score_half(base_ref, g_ref, chat, None, None, w_ref, e_ref, st_ref, acc, pck, tile=tile)
+    blocks, rows = first_ref.shape[0], first_ref.shape[1] // 2
+    side = side_ref[0]
+    mine = firstst_ref[3:4, :]
+    left = jnp.where(side == 0, mine, total)
+    right = jnp.where(side == 0, total, mine)
+    sums = total_rows(jnp.concatenate([left, right], axis=1))
+    for p in range(2 * blocks):
+        pay_ref[p, 2 * rows :, :] = sums
+    for p in range(blocks):
+        pay_ref[2 * p + side, : 2 * rows, :] = first_ref[p]
+        other = 2 * p + 1 - side
+        pay_ref[other, :rows, :] = acc[p * rows : (p + 1) * rows].astype(bf16)
+        pay_ref[other, rows : 2 * rows, :] = pck[p * rows : (p + 1) * rows].astype(bf16)
+
+
+def half_shapes(n, m, d):
+    return [
+        pltpu.VMEM((n, m), bf16),
+        jax.ShapeDtypeStruct((m, d), bf16),
+        jax.ShapeDtypeStruct((8, m), f32),
+    ]
+
+
+def cost(gflops):
+    return pl.CostEstimate(flops=int(gflops * 1e9), bytes_accessed=8 * MIB, transcendentals=0)
+
+
+def first_scores(base, gathered, centers, blocks, tile=512):
     n, d = centers.shape
     m = gathered.shape[0]
+    w, e, st = half_shapes(n, m, d)
+    c = pltpu.VMEM((n, d), bf16)
     return pl.pallas_call(
-        functools.partial(score_kernel, tile=tile, chunk=chunk, iblk=iblk),
+        functools.partial(first_kernel, tile=tile),
         in_specs=[SMEM, VMEM, HBM],
-        out_specs=[VMEM] * 5,
-        out_shape=[
-            pltpu.VMEM((n, m), bf16),
-            pltpu.VMEM((n, d), bf16),
-            jax.ShapeDtypeStruct((m, d), bf16),
-            jax.ShapeDtypeStruct((8, m), f32),
-            jax.ShapeDtypeStruct((groups, 2 * (m // groups) + 8, d), bf16),
-        ],
-        scratch_shapes=[
-            pltpu.VMEM((n, d), bf16),
-            pltpu.SemaphoreType.DMA((n // chunk,)),
-        ],
+        out_specs=[VMEM] * 6,
+        out_shape=[w, c, c, e, st, jax.ShapeDtypeStruct((blocks, 2 * (m // blocks), d), bf16)],
+        scratch_shapes=[pltpu.VMEM((m, d), f32)] * 2 + [pltpu.SemaphoreType.DMA((n // tile,))],
         compiler_params=params(24),
-        name="scores",
+        cost_estimate=cost(6),
+        name="first_scores",
     )(base, gathered, in_hbm(centers))
+
+
+def second_scores(base, side, gathered, chat, first, stats, tile=512):
+    n, d = chat.shape
+    m = gathered.shape[0]
+    blocks, rows = first.shape[0], first.shape[1]
+    w, e, st = half_shapes(n, m, d)
+    return pl.pallas_call(
+        functools.partial(second_kernel, tile=tile),
+        in_specs=[SMEM, SMEM] + [VMEM] * 4,
+        out_specs=[VMEM] * 4,
+        out_shape=[w, e, st, jax.ShapeDtypeStruct((2 * blocks, rows + 8, d), bf16)],
+        scratch_shapes=[pltpu.VMEM((m, d), f32)] * 2,
+        compiler_params=params(24),
+        cost_estimate=cost(6),
+        name="second_scores",
+    )(base, side, gathered, chat, first, stats)
 
 
 def middle_kernel(r_ref, o_ref):
@@ -230,10 +291,12 @@
 
 
 def grad_kernel(
-    own_ref, r_ref, x_ref, st_ref, e_ref, wv, raw, l_ref, xg_ref, o_hbm, out, osem, *, chunk
+    own_ref, side_ref, r_ref, x_ref, sta_ref, stb_ref, ea_ref, eb_ref, wa_ref, wb_ref, raw, l_ref, xg_ref, o_hbm,
+    out, osem, *, chunk
 ):
     n, d = raw.shape
-    m = e_ref.shape[0]
+    half = ea_ref.shape[0]
+    m = 2 * half
     own = x_ref.shape[0]
     chunks = n // chunk
 
@@ -243,15 +306,24 @@
 
     sums = r_ref[...].astype(f32).sum(axis=0)
     total = sums[2 * own :].sum(axis=0, keepdims=True)
-    scale = 1.0 / total
-    coef = st_ref[0:1, :] * (st_ref[1:2, :] * scale - logit_scale)
-    lab1 = st_ref[2:3, :].astype(i32)
+    left, right = 1.0 / total[:, :half], 1.0 / total[:, half:]
+    side = side_ref[0]
+
+    def factors(st_ref, scale):
+        return st_ref[2:3, :].astype(i32), scale, st_ref[0:1, :] * (st_ref[1:2, :] * scale - logit_scale)
+
+    halves = (
+        (ea_ref, wa_ref, *factors(sta_ref, jnp.where(side == 0, left, right))),
+        (eb_ref, wb_ref, *factors(stb_ref, jnp.where(side == 0, right, left))),
+    )
 
     def step(k, _):
         rows = pl.ds(pl.multiple_of(k * chunk, chunk), chunk)
-        hit = lax.broadcasted_iota(i32, (chunk, m), 0) == lab1 - k * chunk
-        share = jnp.where(hit, coef, wv[rows, :].astype(f32) * scale).astype(bf16)
-        grad = dot(share, e_ref[...], 1, 0)
+        row = lax.broadcasted_iota(i32, (chunk, half), 0)
+        grad = 0.0
+        for e_ref, w_ref, lab, scale, coef in halves:
+            share = jnp.where(row == lab - k * chunk, coef, w_ref[rows, :].astype(f32) * scale)
+            grad = grad + dot(share.astype(bf16), e_ref[...], 1, 0)
         w = raw[rows, :].astype(f32)
         inv = inverse_norm(w)
         along = jnp.sum(w * grad, axis=1, keepdims=True) * (inv * inv)
@@ -279,26 +351,22 @@
         save(k).wait()
 
 
-def grads(own_first, received, embeddings, stats, ehat, weighted, centers, chunk=512):
-    n, d = centers.shape
-    m = ehat.shape[0]
+def grads(own_first, side, received, embeddings, stats, ehats, weights, raw, chunk=512):
+    n, d = raw.shape
     own = embeddings.shape[0]
     return pl.pallas_call(
         functools.partial(grad_kernel, chunk=chunk),
-        in_specs=[SMEM] + [VMEM] * 6,
+        in_specs=[SMEM, SMEM] + [VMEM] * 9,
         out_specs=[VMEM, VMEM, HBM],
         out_shape=[
             jax.ShapeDtypeStruct((1, own), f32),
             jax.ShapeDtypeStruct((own, d), f32),
             jax.ShapeDtypeStruct((n, d), f32),
         ],
-        scratch_shapes=[
-            pltpu.VMEM((n, d), f32),
-            pltpu.SemaphoreType.DMA((n // chunk,)),
-        ],
+        scratch_shapes=[pltpu.VMEM((n, d), f32), pltpu.SemaphoreType.DMA((n // chunk,))],
         compiler_params=params(24),
         name="grads",
-    )(own_first, received, embeddings, stats, ehat, weighted, centers)
+    )(own_first, side, received, embeddings, *stats, *ehats, *weights, raw)
 
 
 def exchange(blocks, axis):
@@ -308,21 +376,22 @@
 def per_device(embeddings, labels, centers):
     own, d = embeddings.shape
     n = centers.shape[0]
-    far = lax.axis_size(FAR)
-    near = lax.axis_size(NEAR)
-    m = own * far * near
-    at_near = lax.axis_index(NEAR)
-    at_far = lax.axis_index(FAR)
-    place = lax.axis_index(("x", FAR, "y"))
-    base = (place * n).astype(i32)[None]
-    own_first = ((at_near * far + at_far) * own).astype(i32)[None]
-    embeddings, base, own_first = lax.optimization_barrier((embeddings, base, own_first))
+    far, wide = lax.axis_size(FAR), lax.axis_size("x")
+    at_y = lax.axis_index("y")
+    at = (lax.axis_index("x") * far + lax.axis_index(FAR)) * own
+    half = far * wide * own
+    base = (lax.axis_index(("x", FAR, "y")) * n).astype(i32)[None]
+    own_first = (at_y * half + at).astype(i32)[None]
+    side = at_y.astype(i32)[None]
+    embeddings, base, own_first, side = lax.optimization_barrier((embeddings, base, own_first, side))
     line = exchange(pack(embeddings, labels, far), FAR).reshape(1, far * own, d + LANES)
-    gathered = exchange(jnp.broadcast_to(line, (near, *line.shape[1:])), NEAR)
-    weighted, raw, ehat, stats, pay = scores(base, gathered.reshape(m, d + LANES), centers, near)
-    half = middle(exchange(pay, NEAR), far, own)
+    first = exchange(jnp.broadcast_to(line, (wide, *line.shape[1:])), "x").reshape(half, d + LANES)
+    second = lax.ppermute(first, "y", [(0, 1), (1, 0)])
+    wa, raw, chat, ea, sta, pay = first_scores(base, first, centers, wide)
+    wb, eb, stb, pay = second_scores(base, side, second, chat, pay, sta)
+    received = exchange(middle(exchange(pay, NEAR), far, own), FAR)
     losses, emb_grad, center_grad = grads(
-        own_first, exchange(half, FAR), embeddings, stats, ehat, weighted, raw
+        own_first, side, received, embeddings, (sta, stb), (ea, eb), (wa, wb), raw
     )
     return (losses.reshape(own), emb_grad, center_grad)
 

time: 80.6 us -> 78.9 us (0.979)
  blocking collectives: 60.5 us -> 56.2 us
  Pallas kernels: 19.1 us -> 20.4 us
  starting transfers between devices: 0 us -> 1.28 us
    all_to_all x4, blocking collectives: 60.5 us -> 56.2 us  [exchange(): return lax.all_to_all(blocks, axis, 0, 0, tiled=True)]
    pallas_call x1 -> x2, Pallas kernels: 11.9 us -> 13.2 us  [the longest x1 7.62 us: first_scores(): pl.pallas_call(functools.partial(first_kernel, tile=tile), in_specs=[SMEM...]
    ppermute x0 -> x1, starting transfers between devices: none -> 1.28 us  [per_device(): second = lax.ppermute(first, 'y', [(0, 1), (1, 0)])]
  transfers between devices with their start and end apart: 0 -> 1, of which waited for: 0 -> 0; matrix products, arithmetic and copies ran while one was open for 0% -> 0% of each run, Pallas kernels for 0% -> 10%
where the time goes in v4:
time: 78.9 us; the launch traced here: 78.6 us
  blocking collectives  56.2 us (71%)
  Pallas kernels  20.4 us (26%)
  starting transfers between devices  1.28 us (2%)
    all_to_all x4, blocking collectives, exchange(): return lax.all_to_all(blocks, axis, 0, 0, tiled=True)  56.2 us
    pallas_call x1, Pallas kernels, first_scores(): pl.pallas_call(functools.partial(first_kernel, tile=tile), in_specs=[SMEM...  7.62 us
    pallas_call x1, Pallas kernels, grads(): pl.pallas_call(functools.partial(grad_kernel, chunk=chunk), in_specs=[SME...  6.33 us
    pallas_call x1, Pallas kernels, second_scores(): pl.pallas_call(functools.partial(second_kernel, tile=tile), in_specs=[SME...  5.59 us
  transfers between devices with their start and end apart: 1, of which 0 were waited for; matrix products, arithmetic and copies ran while one was open for 0% of the time, Pallas kernels for 10%

profile of v4, /device:TPU:16, one launch (start us, length us, event | category | flops | bytes accessed | tf_op | source)
XLA Modules:
  0.0 78.6 jit_solution(9487377165790483806)
XLA Ops:
  0.6 0.7 pack.1
  1.4 16.8 %all_to_all.20 = bf16[8,8,640]{2,1,0:T(8,128)(2,1)S(1)} all-to-all(bf16[8,8,640]{2,1,0:T(8,128)(2,1)S(1)} %pack.1), channel_id=1, replica_groups=mesh['x'=4,'z'=8,'y'=2,'dp'=4] {'z'}, dimensions={0} | all-to-all | bytes 163840 | tf_op jit(solution)/shard_map/all_to_all | solution.py:373
  18.2 11.1 %all_to_all.21 = bf16[4,64,640]{2,1,0:T(8,128)(2,1)S(1)} all-to-all(bf16[4,64,640]{2,1,0:T(8,128)(2,1)S(1)} %broadcast_in_dim.20), channel_id=1, replica_groups=mesh['x'=4,'z'=8,'y'=2,'dp'=4] {'x'}, dimensions={0} | all-to-all | bytes 655360 | tf_op jit(solution)/shard_map/all_to_all | solution.py:373
  29.4 1.3 %collective-permute-start = (bf16[256,640]{1,0:T(8,128)(2,1)S(1)}, bf16[256,640]{1,0:T(8,128)(2,1)S(1)}, u32[]{:S(2)}, u32[]{:S(2)}) collective-permute-start(bf16[256,640]{1,0:T(8,128)(2,1)S(1)} %bitcast.6), channel_id=1, source_target_pairs={{0,4},{4,0},{1,5},{5,1},{2,6},{6,2},{3,7},{7,3},{8,12},{12,8},{9,1... | collective-permute-start | bytes 983048 | tf_op jit(solution)/shard_map/ppermute | solution.py:389
  30.6 7.6 %first_scores.1 = (bf16[4096,256]{1,0:T(8,128)(2,1)S(1)}, bf16[4096,512]{1,0:T(8,128)(2,1)S(1)}, bf16[4096,512]{1,0:T(8,128)(2,1)S(1)}, bf16[256,512]{1,0:T(8,12...) custom-call(s32[1]{0:T(128)} %bitcast.base_ref, bf16[256,640]{1,0:T(8,128)(2,1)S(1)} %bitcast.7, ...), custom_call_target="tpu_custom_call" | custom-call | flops 6000000000 | bytes 8388608 | tf_op jit(solution)/shard_map/first_scores/pallas_call | solution.py:239
  38.3 0.0 collective-permute-done.g_ref
  38.3 0.0 copy-start
  38.3 5.6 %second_scores.1 = (bf16[4096,256]{1,0:T(8,128)(2,1)S(1)}, bf16[256,512]{1,0:T(8,128)(2,1)S(1)}, f32[8,256]{1,0:T(8,128)S(1)}, bf16[8,136,512]{2,1,0:T(8,128)(2,1)S(1)}) custom-call(s32[1]{0:T(128)} %bitcast.base_ref, s32[1]{0:T(128)} %bitcast.2.side_ref, bf16[256,640]{1,0:T(8,128)(2,1)S(1)} %collective-permute-done.g_ref, ...), custom_call_target="tpu_custom_call" | custom-call | flops 6000000000 | bytes 8388608 | tf_op jit(solution)/shard_map/second_scores/pallas_call | solution.py:256
  43.9 16.1 %all_to_all.22.r_ref = bf16[8,136,512]{2,1,0:T(8,128)(2,1)S(1)} all-to-all(bf16[8,136,512]{2,1,0:T(8,128)(2,1)S(1)} %get-tuple-element.27), channel_id=1, replica_groups=mesh['x'=4,'z'=8,'y'=2,'dp'=4] {'x','y'}, dimensions={0} | all-to-all | bytes 2228224 | tf_op jit(solution)/shard_map/all_to_all | solution.py:373
  59.9 0.2 middle.1
  60.1 12.2 %all_to_all.23.r_ref = bf16[8,24,512]{2,1,0:T(8,128)(2,1)S(1)} all-to-all(bf16[8,24,512]{2,1,0:T(8,128)(2,1)S(1)} %middle.1), channel_id=1, replica_groups=mesh['x'=4,'z'=8,'y'=2,'dp'=4] {'z'}, dimensions={0} | all-to-all | bytes 393216 | tf_op jit(solution)/shard_map/all_to_all | solution.py:373
  72.3 0.0 copy-done
  72.3 6.3 %grads.1 = (f32[1,8]{1,0:T(1,128)}, f32[8,512]{1,0:T(8,128)}, f32[4096,512]{1,0:T(8,128)}) custom-call(s32[1]{0:T(128)} %bitcast.1.own_ref, s32[1]{0:T(128)} %bitcast.2.side_ref, bf16[8,24,512]{2,1,0:T(8,128)(2,1)S(1)} %all_to_all.23.r_ref, bf16[8,512]{1,0:T(8,128)(2,1)S(1)} %copy-done, f32[8,256]{1,0:T(8,128)S(1)} %get-tuple-element.26.firstst_ref.sta_ref, ...), custom_call_target="tpu_custom_call" | custom-call | tf_op jit(solution)/shard_map/grads/pallas_call | solution.py:357
  (1 shorter events, 0.0 us)
Async XLA Ops:
  29.4 8.9 %collective-permute-start = (bf16[256,640]{1,0:T(8,128)(2,1)S(1)}, bf16[256,640]{1,0:T(8,128)(2,1)S(1)}, u32[]{:S(2)}, u32[]{:S(2)}) collective-permute-start(bf16[256,640]{1,0:T(8,128)(2,1)S(1)} %bitcast.6), channel_id=1, source_target_pairs={{0,4},{4,0},{1,5},{5,1},{2,6},{6,2},{3,7},{7,3},{8,12},{12,8},{9,1... | collective-permute-start | bytes 983048 | tf_op jit(solution)/shard_map/ppermute | solution.py:389
  38.3 34.0 %copy-start = (bf16[8,512]{1,0:T(8,128)(2,1)S(1)}, bf16[8,512]{1,0:T(8,128)(2,1)}, u32[]{:S(2)}) copy-start(bf16[8,512]{1,0:T(8,128)(2,1)} %x_ref) | copy-start | bytes 24580
